TPU v7x, 512 devices: a whole 4x8x8 slice. The times are simulated.
512 devices in a mesh: slab: 128 (over z, y, core), sub: 4 (over x).
Axes of the slice: x: 4, y: 8, z: 8, core: 2. Of those that a mesh axis runs over, the one named last changes fastest.
Arguments:
- populations: float32 [19, 128, 128, 128], P(None, 'slab', 'sub'), may hold values from 0.5 to 1.5
- marker_cell: int32 [128, 4, 256, 128], P('slab', 'sub'), may hold values from 0 to 4095
- marker_count: int32 [128, 4, 256], P('slab', 'sub'), may hold values from 1 to 128
- particle_count: int32 [128, 4], P('slab', 'sub'), may hold values from 32 to 256, as said below
- particle_id: int32 [128, 4, 256], P('slab', 'sub'), may hold values from 0 to 32767, as said below
- owner_table: int32 [4, 128], P('sub'), may hold values from 0 to 127, as said below
- particle_velocity: float32 [128, 4, 3, 256], P('slab', 'sub'), may hold values from -0.3 to 0.3
- pair_list: int32 [128, 4, 256, 4], P('slab', 'sub'), may hold values from 0 to 255, as said below
- pair_gap: float32 [128, 4, 256, 4], P('slab', 'sub'), may hold values from 0.25 to 4
- self_coupling: bfloat16 [128, 128], replicated, may hold values from -2 to 16
- pair_coupling: bfloat16 [128, 128], replicated, may hold values from -1 to 6
Outputs:
- read: float32 [19, 128, 128, 128], P(None, 'slab', 'sub')
- marker_force: bfloat16 [128, 4, 256, 3, 128], P('slab', 'sub')
Inputs may be any that keep to these rules, and one draw needn't show every extreme that they name: `particle_count`: A holder's live particles fill its first slots; in every sub index some holder has 256 live particles. `particle_id`: live slots of one sub index hold distinct ids; a live slot's particle is owned by slab index owner_table[j, id // 256] of the same sub index j. At most 2 live particles of one holder belong to one owner, and in every draw some holder sends exactly 2 to every owner. Dead slots hold arbitrary ids. `owner_table`: each row is a permutation of the slab indices. `pair_list`: A spot never names itself.
All inputs are finite; a program needn't handle non-finite values.
Results may differ from a plain program's by a relative error of at most 0.0053.
Values may be sent and summed in bfloat16 or wider, within the bound.
A program may use at most 64 MiB of HBM per device.

v0:
```python
import math

import jax
import jax.numpy as jnp
from jax import lax
from jax.sharding import PartitionSpec as P

lattice_dirs = [
    (0, 0, 0),
    (1, 0, 0),
    (-1, 0, 0),
    (0, 1, 0),
    (0, -1, 0),
    (0, 0, 1),
    (0, 0, -1),
    (1, 1, 0),
    (-1, -1, 0),
    (1, -1, 0),
    (-1, 1, 0),
    (1, 0, 1),
    (-1, 0, -1),
    (1, 0, -1),
    (-1, 0, 1),
    (0, 1, 1),
    (0, -1, -1),
    (0, 1, -1),
    (0, -1, 1),
]
lattice_weights = [1.0 / 3.0] + [1.0 / 18.0] * 6 + [1.0 / 36.0] * 12
opposite_of = [0, 2, 1, 4, 3, 6, 5, 8, 7, 10, 9, 12, 11, 14, 13, 16, 15, 18, 17]
relax_rate = 1.25
marker_block_most = 4096


def extended(block, sides, width, periodic):
    for axis, dim in sides:
        count = lax.axis_size(axis)
        forward = [(i, i + 1) for i in range(count - 1)]
        if periodic:
            forward.append((count - 1, 0))
        backward = [(target, source) for source, target in forward]
        low = lax.ppermute(
            lax.slice_in_dim(block, block.shape[dim] - width, None, axis=dim), axis, forward
        )
        high = lax.ppermute(lax.slice_in_dim(block, 0, width, axis=dim), axis, backward)
        block = jnp.concatenate([low, block, high], axis=dim)
    return block


def moments(populations):
    dirs_table = jnp.array(lattice_dirs, jnp.float32)
    density = jnp.sum(populations, axis=0)
    moment = jnp.einsum("ic,i...->c...", dirs_table, populations, precision=lax.Precision.HIGHEST)
    return (density, moment)


def collide(populations, density, moment, body_force):
    dirs_table = jnp.array(lattice_dirs, jnp.float32)
    weight_col = jnp.array(lattice_weights, jnp.float32).reshape(
        (19,) + (1,) * (populations.ndim - 1)
    )
    velocity = (moment + 0.5 * body_force) / density
    along = jnp.einsum("ic,c...->i...", dirs_table, velocity, precision=lax.Precision.HIGHEST)
    push = jnp.einsum("ic,c...->i...", dirs_table, body_force, precision=lax.Precision.HIGHEST)
    speed_sq = jnp.sum(velocity * velocity, axis=0)
    work_rate = jnp.sum(velocity * body_force, axis=0)
    equilibrium = weight_col * density * (1.0 + 3.0 * along + 4.5 * along * along - 1.5 * speed_sq)
    source = (1.0 - 0.5 * relax_rate) * weight_col * (3.0 * (push - work_rate) + 9.0 * along * push)
    return populations - relax_rate * (populations - equilibrium) + source


def lubricate(owned, partner_index, partner_gap, self_coupling, pair_coupling):
    marker_width = owned.shape[-1]
    partners = owned[partner_index]
    weighted = jnp.sum(partners.astype(jnp.float32) / partner_gap[:, :, None, None], axis=1).astype(
        jnp.bfloat16
    )
    direct = jnp.dot(
        owned.reshape(-1, marker_width), self_coupling, preferred_element_type=jnp.float32
    )
    coupled = jnp.dot(
        weighted.reshape(-1, marker_width), pair_coupling, preferred_element_type=jnp.float32
    )
    return (direct + coupled).astype(jnp.bfloat16).reshape(owned.shape)


def cell_picks(cells, row_total, cell_depth, pick_type):
    row_pick = (cells // cell_depth)[:, None] == jnp.arange(row_total, dtype=jnp.int32)[None, :]
    depth_pick = (cells % cell_depth)[:, None] == jnp.arange(cell_depth, dtype=jnp.int32)[None, :]
    return (row_pick.astype(pick_type), depth_pick)


def sample_markers(flow_field, flat_cells, row_total, cell_depth, block_size):

    def sample_block(cells):
        row_pick, depth_pick = cell_picks(cells, row_total, cell_depth, jnp.float32)
        picked_rows = jnp.dot(
            row_pick,
            flow_field,
            precision=lax.Precision.HIGHEST,
            preferred_element_type=jnp.float32,
        ).reshape(block_size, 3, cell_depth)
        return jnp.sum(jnp.where(depth_pick[:, None, :], picked_rows, 0.0), axis=2)

    return lax.map(sample_block, flat_cells.reshape(-1, block_size)).reshape(-1, 3)


def spread_markers(force_terms, flat_cells, row_total, cell_depth, block_size):

    def spread_block(total, operands):
        cells, terms = operands
        row_pick, depth_pick = cell_picks(cells, row_total, cell_depth, jnp.bfloat16)
        placed = jnp.where(depth_pick[:, None, :], terms[:, :, None], jnp.zeros((), jnp.bfloat16))
        placed = placed.reshape(block_size, 3 * cell_depth)
        part_sum = lax.dot_general(
            row_pick, placed, (((0,), (0,)), ((), ())), preferred_element_type=jnp.float32
        )
        return (total + part_sum, None)

    start = jnp.zeros((row_total, 3 * cell_depth), jnp.float32)
    total, unused = lax.scan(
        spread_block,
        start,
        (flat_cells.reshape(-1, block_size), force_terms.reshape(-1, block_size, 3)),
    )
    return total


def stream_block(padded, collided, sub_position, sub_total):
    planes, rows_y = (collided.shape[1], collided.shape[2])
    outputs = []
    for number in range(19):
        step_x, step_y, step_z = lattice_dirs[number]
        moved = padded[
            number, 1 - step_x : 1 - step_x + planes, 1 - step_y : 1 - step_y + rows_y, :
        ]
        moved = jnp.roll(moved, step_z, axis=2)
        if step_y != 0:
            edge_row = 0 if step_y == 1 else rows_y - 1
            wall_device = sub_position == (0 if step_y == 1 else sub_total - 1)
            at_wall = (jnp.arange(rows_y) == edge_row)[None, :, None] & wall_device
            moved = jnp.where(at_wall, collided[opposite_of[number]], moved)
        outputs.append(moved)
    return jnp.stack(outputs)


def per_device(
    populations,
    marker_cell,
    marker_count,
    particle_count,
    particle_id,
    owner_table,
    particle_velocity,
    pair_list,
    pair_gap,
    self_coupling,
    pair_coupling,
):
    slab_count = lax.axis_size("slab")
    cell_index = marker_cell[0, 0]
    slot_count, marker_width = cell_index.shape
    capacity = slot_count // slab_count
    buffer_rows = slab_count * capacity
    cell_depth = populations.shape[3]
    row_total = populations.shape[1] * populations.shape[2]
    marker_total = slot_count * marker_width
    block_size = math.gcd(marker_total, marker_block_most)
    density, moment = moments(populations)
    fluid_flow = (moment / density).reshape(3, row_total, cell_depth)
    flow_field = jnp.transpose(fluid_flow, (1, 0, 2)).reshape(row_total, 3 * cell_depth)
    flat_cells = cell_index.reshape(-1)
    sampled = sample_markers(flow_field, flat_cells, row_total, cell_depth, block_size)
    sampled = jnp.transpose(sampled.reshape(slot_count, marker_width, 3), (0, 2, 1))
    slot_index = jnp.arange(slot_count, dtype=jnp.int32)
    alive_slot = slot_index < particle_count[0, 0]
    marker_index = jnp.arange(marker_width, dtype=jnp.int32)
    live_marker = alive_slot[:, None] & (marker_index[None, :] < marker_count[0, 0][:, None])
    target_speed = jnp.transpose(particle_velocity[0, 0])[:, :, None]
    slip_value = jnp.where(live_marker[:, None, :], target_speed - sampled, 0.0).astype(
        jnp.bfloat16
    )
    identities = particle_id[0, 0]
    slab_range = jnp.arange(slab_count, dtype=jnp.int32)
    range_match = (identities // slot_count)[:, None] == slab_range[None, :]
    owner_slab = jnp.sum(jnp.where(range_match, owner_table[0][None, :], 0), axis=1)
    chosen = ((owner_slab[:, None] == slab_range[None, :]) & alive_slot[:, None]).astype(jnp.int32)
    earlier = jnp.cumsum(chosen, axis=0) - chosen
    position = jnp.sum(earlier * chosen, axis=1)
    send_row = jnp.where(alive_slot, owner_slab * capacity + position, buffer_rows)
    out_slip = (
        jnp.zeros((buffer_rows, 3, marker_width), jnp.bfloat16)
        .at[send_row]
        .set(slip_value, mode="drop")
    )
    out_spot = (
        jnp.full((buffer_rows,), -1, jnp.int32)
        .at[send_row]
        .set(identities % slot_count, mode="drop")
    )
    got_slip, got_spot = (
        lax.all_to_all(
            out_slip.reshape(slab_count, capacity, 3, marker_width),
            "slab",
            split_axis=0,
            concat_axis=0,
            tiled=True,
        ),
        lax.all_to_all(
            out_spot.reshape(slab_count, capacity), "slab", split_axis=0, concat_axis=0, tiled=True
        ),
    )
    got_spot = got_spot.reshape(-1)
    landing = jnp.where(got_spot >= 0, got_spot, slot_count)
    owned = (
        jnp.zeros((slot_count, 3, marker_width), jnp.bfloat16)
        .at[landing]
        .set(got_slip.reshape(-1, 3, marker_width), mode="drop")
    )
    correction = lubricate(owned, pair_list[0, 0], pair_gap[0, 0], self_coupling, pair_coupling)
    reply_rows = correction[jnp.minimum(landing, slot_count - 1)]
    returned = lax.all_to_all(
        reply_rows.reshape(slab_count, capacity, 3, marker_width),
        "slab",
        split_axis=0,
        concat_axis=0,
        tiled=True,
    )
    own_rows = returned.reshape(buffer_rows, 3, marker_width)[
        jnp.minimum(send_row, buffer_rows - 1)
    ]
    marker_force = jnp.where(live_marker[:, None, :], own_rows, 0.0)
    force_terms = jnp.transpose(marker_force, (0, 2, 1)).reshape(marker_total, 3)
    force_rows = spread_markers(force_terms, flat_cells, row_total, cell_depth, block_size)
    body_force = jnp.transpose(force_rows.reshape(row_total, 3, cell_depth), (1, 0, 2)).reshape(
        moment.shape
    )
    collided = collide(populations, density, moment, body_force)
    widened = extended(collided, (("slab", 1),), 1, True)
    padded = extended(widened, (("sub", 2),), 1, False)
    read = stream_block(padded, collided, lax.axis_index("sub"), lax.axis_size("sub"))
    return (read, marker_force[None, None])


def solution(mesh):
    placed = (
        P(None, "slab", "sub", None),
        P("slab", "sub", None, None),
        P("slab", "sub", None),
        P("slab", "sub"),
        P("slab", "sub", None),
        P("sub", None),
        P("slab", "sub", None, None),
        P("slab", "sub", None, None),
        P("slab", "sub", None, None),
        P(),
        P(),
    )
    return jax.shard_map(
        per_device,
        mesh=mesh,
        in_specs=placed,
        out_specs=(P(None, "slab", "sub", None), P("slab", "sub", None, None, None)),
        check_vma=False,
    )
```

profile of v0, /device:TPU:6, one launch (start us, length us, event | category | flops | bytes accessed | tf_op | source)
XLA Modules:
  0.0 196.8 jit_solution(4310434636152105539)
XLA Ops:
  1.3 0.8 select_reduce_fusion.1
  3.7 1.4 scatter_custom_fusion
  5.8 17.8 %all-to-all-start = ((s32[128,1,2]{2,1,0:T(1,128)}), s32[128,1,2]{2,1,0:T(1,128)S(1)}, u32[]{:S(2)}, u32[]{:S(2)}) async-start(s32[128,1,2]{2,1,0:T(1,128)} %bitcast.15), calls=%async_computation | async-start | bytes 131072 | tf_op jit(solution)/shard_map/all_to_all | solution.py:209
  24.5 1.0 reduce_sum.66
  25.5 2.1 %broadcast_divide_fusion = (f32[3,32,128]{2,0,1:T(4,128)S(1)}, f32[3,32,128]{2,0,1:T(4,128)}) fusion(f32[32,128]{1,0:T(8,128)S(1)} %reduce_sum.66, f32[19,3,1]{0,1,2:T(4,128)} %constant.207, f32[19,32,128]{2,1,0:T(8,128)} %bitcast.190), kind=kOutput, calls=%fused_computation.99 | convolution fusion | flops 2813952 | bytes 426212 | tf_op jit(solution)/shard_map/ic,i...->c.../dot_general | solution.py:53
  27.6 1.6 reshape_reshape_squeeze.4
  29.2 37.7 %while.25 = (s32[]{:T(128)}, f32[8,4096,3]{1,2,0:T(4,128)S(1)}, s32[8,4096]{1,0:T(8,128)}, f32[32,384]{1,0:T(8,128)S(1)}, s32[]{:T(128)}) while((s32[]{:T(128)}, f32[8,4096,3]{1,2,0:T(4,128)S(1)}, s32[8,4096]{1,0:T(8,128)}, f32[32,384]{1,0:T(8,128)S(1)}, s32[]{:T(128)}) %tuple.100), condition=%wide.region_8.9_spmd, body=%wide.region_6.8_spmd.sunk | while | flops 607846400 | bytes 13975621 | solution.py:105
  29.2 0.9 constant_dynamic-slice_fusion.4
  30.2 2.7 %fusion.54 = f32[4096,384]{0,1:T(8,128)S(1)} fusion(f32[32,384]{1,0:T(8,128)S(1)} %get-tuple-element.294, s32[4096]{0:T(1024)S(1)} %get-tuple-element.273), kind=kOutput, calls=%fused_computation.9.clone.1 | convolution fusion | flops 604110848 | bytes 6356992 | tf_op jit(solution)/shard_map/while/body/eval_jaxpr/dot_general | solution.py:97
  33.9 0.9 constant_dynamic-slice_fusion.4
  34.9 2.7 %fusion.54 = f32[4096,384]{0,1:T(8,128)S(1)} fusion(f32[32,384]{1,0:T(8,128)S(1)} %get-tuple-element.294, s32[4096]{0:T(1024)S(1)} %get-tuple-element.273), kind=kOutput, calls=%fused_computation.9.clone.1 | convolution fusion | flops 604110848 | bytes 6356992 | tf_op jit(solution)/shard_map/while/body/eval_jaxpr/dot_general | solution.py:97
  38.7 0.9 constant_dynamic-slice_fusion.4
  39.6 2.7 %fusion.54 = f32[4096,384]{0,1:T(8,128)S(1)} fusion(f32[32,384]{1,0:T(8,128)S(1)} %get-tuple-element.294, s32[4096]{0:T(1024)S(1)} %get-tuple-element.273), kind=kOutput, calls=%fused_computation.9.clone.1 | convolution fusion | flops 604110848 | bytes 6356992 | tf_op jit(solution)/shard_map/while/body/eval_jaxpr/dot_general | solution.py:97
  43.4 0.9 constant_dynamic-slice_fusion.4
  44.3 2.7 %fusion.54 = f32[4096,384]{0,1:T(8,128)S(1)} fusion(f32[32,384]{1,0:T(8,128)S(1)} %get-tuple-element.294, s32[4096]{0:T(1024)S(1)} %get-tuple-element.273), kind=kOutput, calls=%fused_computation.9.clone.1 | convolution fusion | flops 604110848 | bytes 6356992 | tf_op jit(solution)/shard_map/while/body/eval_jaxpr/dot_general | solution.py:97
  48.1 0.9 constant_dynamic-slice_fusion.4
  49.0 2.7 %fusion.54 = f32[4096,384]{0,1:T(8,128)S(1)} fusion(f32[32,384]{1,0:T(8,128)S(1)} %get-tuple-element.294, s32[4096]{0:T(1024)S(1)} %get-tuple-element.273), kind=kOutput, calls=%fused_computation.9.clone.1 | convolution fusion | flops 604110848 | bytes 6356992 | tf_op jit(solution)/shard_map/while/body/eval_jaxpr/dot_general | solution.py:97
  52.8 0.9 constant_dynamic-slice_fusion.4
  53.7 2.7 %fusion.54 = f32[4096,384]{0,1:T(8,128)S(1)} fusion(f32[32,384]{1,0:T(8,128)S(1)} %get-tuple-element.294, s32[4096]{0:T(1024)S(1)} %get-tuple-element.273), kind=kOutput, calls=%fused_computation.9.clone.1 | convolution fusion | flops 604110848 | bytes 6356992 | tf_op jit(solution)/shard_map/while/body/eval_jaxpr/dot_general | solution.py:97
  57.5 0.9 constant_dynamic-slice_fusion.4
  58.4 2.7 %fusion.54 = f32[4096,384]{0,1:T(8,128)S(1)} fusion(f32[32,384]{1,0:T(8,128)S(1)} %get-tuple-element.294, s32[4096]{0:T(1024)S(1)} %get-tuple-element.273), kind=kOutput, calls=%fused_computation.9.clone.1 | convolution fusion | flops 604110848 | bytes 6356992 | tf_op jit(solution)/shard_map/while/body/eval_jaxpr/dot_general | solution.py:97
  62.2 0.9 constant_dynamic-slice_fusion.4
  63.1 2.7 %fusion.54 = f32[4096,384]{0,1:T(8,128)S(1)} fusion(f32[32,384]{1,0:T(8,128)S(1)} %get-tuple-element.294, s32[4096]{0:T(1024)S(1)} %get-tuple-element.273), kind=kOutput, calls=%fused_computation.9.clone.1 | convolution fusion | flops 604110848 | bytes 6356992 | tf_op jit(solution)/shard_map/while/body/eval_jaxpr/dot_general | solution.py:97
  67.5 7.0 %scatter_fusion = bf16[256,3,128]{2,1,0:T(4,128)(2,1)S(1)} fusion(bf16[256,3,128]{2,1,0:T(4,128)(2,1)S(1)} %broadcast.561.clone, s32[256]{0:T(256)S(1)} %bitcast.211, bf16[256,3,128]{2,1,0:T(4,128)(2,1)S(1)} %fusion.19), kind=kCustom, calls=%fused_computation.4 | custom fusion | bytes 590848 | tf_op jit(solution)/shard_map/scatter | solution.py:194
  74.5 0.8 copy.366
  75.6 14.3 %all-to-all-start.1 = ((bf16[128,2,3,128]{3,1,2,0:T(2,128)(2,1)}), bf16[128,2,3,128]{3,1,2,0:T(2,128)(2,1)S(1)}, u32[]{:S(2)}, u32[]{:S(2)}) async-start(bf16[128,2,3,128]{3,1,2,0:T(2,128)(2,1)} %copy.366), calls=%async_computation.1 | async-start | bytes 393216 | tf_op jit(solution)/shard_map/all_to_all | solution.py:202
  91.5 11.6 %all-to-all-done.1 = bf16[128,2,3,128]{3,1,2,0:T(2,128)(2,1)S(1)} async-done(((bf16[128,2,3,128]{3,1,2,0:T(2,128)(2,1)}), bf16[128,2,3,128]{3,1,2,0:T(2,128)(2,1)S(1)}, u32[]{:S(2)}, u32[]{:S(2)}) %all-to-all-start.1) | async-done | bytes 196640 | tf_op jit(solution)/shard_map/all_to_all | solution.py:202
  103.3 7.3 %scatter_fusion.1 = bf16[256,3,128]{2,1,0:T(4,128)(2,1)S(1)} fusion(bf16[256,3,128]{2,1,0:T(4,128)(2,1)S(1)} %broadcast.561, s32[256]{0:T(256)S(1)} %bitcast.212, bf16[256,3,128]{2,1,0:T(4,128)(2,1)S(1)} %bitcast.194), kind=kCustom, calls=%fused_computation.5 | custom fusion | bytes 590848 | tf_op jit(solution)/shard_map/scatter | solution.py:218
  110.8 3.6 %gather_fusion = bf16[1024,3,128]{2,1,0:T(4,128)(2,1)S(1)} fusion(bf16[256,3,128]{2,1,0:T(4,128)(2,1)S(1)} %scatter_fusion.1, s32[1024]{0:T(1024)S(1)} %broadcast_clamp_fusion), kind=kCustom, calls=%fused_computation | custom fusion | bytes 1576960 | tf_op jit(solution)/shard_map/gather | solution.py:74
  114.4 1.7 fusion.7
  116.8 1.0 gather_fusion.1
  117.7 0.8 copy.370
  118.6 6.2 %all-to-all-start.2 = ((bf16[128,2,3,128]{3,1,2,0:T(2,128)(2,1)}), bf16[128,2,3,128]{3,1,2,0:T(2,128)(2,1)S(1)}, u32[]{:S(2)}, u32[]{:S(2)}) async-start(bf16[128,2,3,128]{3,1,2,0:T(2,128)(2,1)} %copy.370), calls=%async_computation.2 | async-start | bytes 393216 | tf_op jit(solution)/shard_map/all_to_all | solution.py:222
  125.9 12.3 %all-to-all-done.2 = bf16[128,2,3,128]{3,1,2,0:T(2,128)(2,1)S(1)} async-done(((bf16[128,2,3,128]{3,1,2,0:T(2,128)(2,1)}), bf16[128,2,3,128]{3,1,2,0:T(2,128)(2,1)S(1)}, u32[]{:S(2)}, u32[]{:S(2)}) %all-to-all-start.2) | async-done | bytes 196640 | tf_op jit(solution)/shard_map/all_to_all | solution.py:222
  138.5 1.0 gather_fusion.2
  139.6 0.9 broadcast_select_fusion.1
  140.5 28.6 %while.26 = (s32[]{:T(128)}, f32[32,384]{1,0:T(8,128)S(1)}, s32[8,4096]{1,0:T(8,128)}, bf16[8,4096,3]{1,2,0:T(4,128)(2,1)}, s32[]{:T(128)}, /*index=5*/s32[]{:T(128)}) while((s32[]{:T(128)}, f32[32,384]{1,0:T(8,128)S(1)}, s32[8,4096]{1,0:T(8,128)}, bf16[8,4096,3]{1,2,0:T(4,128)(2,1)}, s32[]{:T(128)}, /*index=5*/s32[]{:T(128)}) %tuple.97), condition=%wide.region_13.14_spmd.clone, body=%wide.region_12.13_spmd.clone.sunk | while | flops 102993920 | bytes 7626839 | solution.py:121
  140.5 1.0 constant_dynamic-slice_fusion.5
  143.0 1.0 convolution_add_fusion.3
  144.1 0.9 constant_dynamic-slice_fusion.5
  146.6 1.0 convolution_add_fusion.3
  147.7 0.9 constant_dynamic-slice_fusion.5
  150.2 1.0 convolution_add_fusion.3
  151.3 0.9 constant_dynamic-slice_fusion.5
  153.8 1.0 convolution_add_fusion.3
  154.8 0.9 constant_dynamic-slice_fusion.5
  157.3 1.0 convolution_add_fusion.3
  158.4 0.9 constant_dynamic-slice_fusion.5
  160.9 1.0 convolution_add_fusion.3
  162.0 0.9 constant_dynamic-slice_fusion.5
  164.5 1.0 convolution_add_fusion.3
  165.6 0.9 constant_dynamic-slice_fusion.5
  168.1 1.0 convolution_add_fusion.3
  169.2 1.2 fusion.27
  170.4 1.0 multiply_reduce_fusion
  171.4 1.2 fusion.39
  172.6 1.0 fusion.18
  173.6 2.0 %collective-permute-start = (f32[19,1,32,128]{3,2,1,0:T(8,128)S(1)}, f32[19,1,32,128]{3,2,1,0:T(8,128)S(1)}, u32[]{:S(2)}, u32[]{:S(2)}) collective-permute-start(f32[19,1,32,128]{3,2,1,0:T(8,128)S(1)} %fusion.18), channel_id=1, source_target_pairs={{0,4},{4,8},{8,12},{12,16},{16,20},{20,24},{24,28},{28,32},{32,36}... | collective-permute-start | bytes 933896 | tf_op jit(solution)/shard_map/ppermute | solution.py:42
  175.7 6.9 %collective-permute-start.1 = (f32[19,1,32,128]{3,2,1,0:T(8,128)S(1)}, f32[19,1,32,128]{3,2,1,0:T(8,128)S(1)}, u32[]{:S(2)}, u32[]{:S(2)}) collective-permute-start(f32[19,1,32,128]{3,2,1,0:T(8,128)S(1)} %fusion.18), channel_id=1, source_target_pairs={{4,0},{8,4},{12,8},{16,12},{20,16},{24,20},{28,24},{32,28},{36,32}... | collective-permute-start | bytes 933896 | tf_op jit(solution)/shard_map/ppermute | solution.py:45
  182.5 1.2 bitcast_select_fusion
  185.2 1.8 collective-permute-done.1
  187.0 1.3 collective-permute-start.2
  188.3 4.5 %collective-permute-start.3 = (f32[19,3,1,128]{3,2,1,0:T(1,128)S(1)}, f32[19,3,1,128]{3,2,1,0:T(1,128)S(1)}, u32[]{:S(2)}, u32[]{:S(2)}) collective-permute-start(f32[19,3,1,128]{3,2,1,0:T(1,128)S(1)} %get-tuple-element.204), channel_id=1, source_target_pairs={{1,0},{2,1},{3,2},{5,4},{6,5},{7,6},{9,8},{10,9},{11,10},{13,12},{... | collective-permute-start | bytes 87560 | tf_op jit(solution)/shard_map/ppermute | solution.py:45
  193.1 1.3 collective-permute-done.3
  (172 shorter events, 33.2 us)
Async XLA Ops:
  0.6 115.6 %copy-start = (bf16[128,128]{1,0:T(8,128)(2,1)S(1)}, bf16[128,128]{1,0:T(8,128)(2,1)}, u32[]{:S(2)}) copy-start(bf16[128,128]{1,0:T(8,128)(2,1)} %param.27) | copy-start | bytes 98308
  5.8 69.8 %all-to-all-start = ((s32[128,1,2]{2,1,0:T(1,128)}), s32[128,1,2]{2,1,0:T(1,128)S(1)}, u32[]{:S(2)}, u32[]{:S(2)}) async-start(s32[128,1,2]{2,1,0:T(1,128)} %bitcast.15), calls=%async_computation | async-start | bytes 131072 | tf_op jit(solution)/shard_map/all_to_all | solution.py:209
  24.5 115.1 %copy-start.3 = (pred[256,128]{1,0:T(8,128)(4,1)}, pred[256,128]{1,0:T(8,128)(4,1)S(1)}, u32[]{:S(2)}) copy-start(pred[256,128]{1,0:T(8,128)(4,1)S(1)} %fusion.24) | copy-start | bytes 98308
  25.5 2.1 %copy-start.4 = (f32[32,128]{1,0:T(8,128)}, f32[32,128]{1,0:T(8,128)S(1)}, u32[]{:S(2)}) copy-start(f32[32,128]{1,0:T(8,128)S(1)} %reduce_sum.66) | copy-start | bytes 49156
  29.2 37.7 %copy-start.10 = (f32[1,1,3,256]{3,1,2,0:T(1,128)S(1)}, f32[1,1,3,256]{3,1,2,0:T(1,128)}, u32[]{:S(2)}) copy-start(f32[1,1,3,256]{3,1,2,0:T(1,128)} %param.24) | copy-start | bytes 9220
  29.2 38.2 %copy-start.9 = (s32[1,1,256,4]{2,3,1,0:T(4,128)S(1)}, s32[1,1,256,4]{2,3,1,0:T(4,128)}, u32[]{:S(2)}) copy-start(s32[1,1,256,4]{2,3,1,0:T(4,128)} %param.25) | copy-start | bytes 12292
  67.5 22.4 %copy-start.8 = (f32[1,1,256,4]{2,3,1,0:T(4,128)S(1)}, f32[1,1,256,4]{2,3,1,0:T(4,128)}, u32[]{:S(2)}) copy-start(f32[1,1,256,4]{2,3,1,0:T(4,128)} %param.26) | copy-start | bytes 12292
  75.6 27.5 %all-to-all-start.1 = ((bf16[128,2,3,128]{3,1,2,0:T(2,128)(2,1)}), bf16[128,2,3,128]{3,1,2,0:T(2,128)(2,1)S(1)}, u32[]{:S(2)}, u32[]{:S(2)}) async-start(bf16[128,2,3,128]{3,1,2,0:T(2,128)(2,1)} %copy.366), calls=%async_computation.1 | async-start | bytes 393216 | tf_op jit(solution)/shard_map/all_to_all | solution.py:202
  103.2 13.2 %copy-start.5 = (bf16[128,128]{1,0:T(8,128)(2,1)S(1)}, bf16[128,128]{1,0:T(8,128)(2,1)}, u32[]{:S(2)}) copy-start(bf16[128,128]{1,0:T(8,128)(2,1)} %param.28) | copy-start | bytes 98308
  118.6 19.6 %all-to-all-start.2 = ((bf16[128,2,3,128]{3,1,2,0:T(2,128)(2,1)}), bf16[128,2,3,128]{3,1,2,0:T(2,128)(2,1)S(1)}, u32[]{:S(2)}, u32[]{:S(2)}) async-start(bf16[128,2,3,128]{3,1,2,0:T(2,128)(2,1)} %copy.370), calls=%async_computation.2 | async-start | bytes 393216 | tf_op jit(solution)/shard_map/all_to_all | solution.py:222
  139.5 0.9 copy-start.2
  140.5 32.2 %copy-start.1 = (f32[19,1,32,128]{3,2,1,0:T(8,128)S(1)}, f32[19,1,32,128]{3,2,1,0:T(8,128)}, u32[]{:S(2)}) copy-start(f32[19,1,32,128]{3,2,1,0:T(8,128)} %param.18) | copy-start | bytes 933892
  169.1 23.7 %copy-start.6 = (pred[32]{0:T(512)(128)(4,1)S(1)}, pred[32]{0:T(512)(128)(4,1)}, u32[]{:S(2)}) copy-start(pred[32]{0:T(512)(128)(4,1)} %compare_and_fusion.1) | copy-start | bytes 100
  169.1 25.2 %copy-start.7 = (pred[32]{0:T(512)(128)(4,1)S(1)}, pred[32]{0:T(512)(128)(4,1)}, u32[]{:S(2)}) copy-start(pred[32]{0:T(512)(128)(4,1)} %compare_and_fusion) | copy-start | bytes 100
  173.6 11.5 %collective-permute-start = (f32[19,1,32,128]{3,2,1,0:T(8,128)S(1)}, f32[19,1,32,128]{3,2,1,0:T(8,128)S(1)}, u32[]{:S(2)}, u32[]{:S(2)}) collective-permute-start(f32[19,1,32,128]{3,2,1,0:T(8,128)S(1)} %fusion.18), channel_id=1, source_target_pairs={{0,4},{4,8},{8,12},{12,16},{16,20},{20,24},{24,28},{28,32},{32,36}... | collective-permute-start | bytes 933896 | tf_op jit(solution)/shard_map/ppermute | solution.py:42
  175.7 11.3 %collective-permute-start.1 = (f32[19,1,32,128]{3,2,1,0:T(8,128)S(1)}, f32[19,1,32,128]{3,2,1,0:T(8,128)S(1)}, u32[]{:S(2)}, u32[]{:S(2)}) collective-permute-start(f32[19,1,32,128]{3,2,1,0:T(8,128)S(1)} %fusion.18), channel_id=1, source_target_pairs={{4,0},{8,4},{12,8},{16,12},{20,16},{24,20},{28,24},{32,28},{36,32}... | collective-permute-start | bytes 933896 | tf_op jit(solution)/shard_map/ppermute | solution.py:45
  187.0 5.9 %collective-permute-start.2 = (f32[19,3,1,128]{3,2,1,0:T(1,128)S(1)}, f32[19,3,1,128]{3,2,1,0:T(1,128)S(1)}, u32[]{:S(2)}, u32[]{:S(2)}) collective-permute-start(f32[19,3,1,128]{3,2,1,0:T(1,128)S(1)} %get-tuple-element.205), channel_id=1, source_target_pairs={{0,1},{1,2},{2,3},{4,5},{5,6},{6,7},{8,9},{9,10},{10,11},{12,13},{... | collective-permute-start | bytes 87560 | tf_op jit(solution)/shard_map/ppermute | solution.py:42
  188.3 6.1 %collective-permute-start.3 = (f32[19,3,1,128]{3,2,1,0:T(1,128)S(1)}, f32[19,3,1,128]{3,2,1,0:T(1,128)S(1)}, u32[]{:S(2)}, u32[]{:S(2)}) collective-permute-start(f32[19,3,1,128]{3,2,1,0:T(1,128)S(1)} %get-tuple-element.204), channel_id=1, source_target_pairs={{1,0},{2,1},{3,2},{5,4},{6,5},{7,6},{9,8},{10,9},{11,10},{13,12},{... | collective-permute-start | bytes 87560 | tf_op jit(solution)/shard_map/ppermute | solution.py:45
  196.1 0.7 copy-start.11
where the time goes:
time: 200 us; the launch traced here: 197 us
  starting transfers between devices  53 us (26%)
  local copies, waits for them, and re-layouts  51 us (26%)
  matrix products  34.5 us (17%)
  other arithmetic  28 us (14%)
  waiting for transfers between devices  27.7 us (14%)
    dot_general x8, matrix products, sample_block(): jnp.dot(row_pick, flow_field, precision=lax.Precision.HIGHEST, preferred_...  21.3 us
    all_to_all x1, starting transfers between devices, per_device(): lax.all_to_all(out_spot.reshape(slab_count, capacity), 'slab', split_axis...  17.8 us
    dynamic_slice x16, local copies, waits for them, and re-layouts, sample_markers(): lax.map(sample_block, flat_cells.reshape(-1, block_size)).reshape(-1, 3)  14.8 us
    all_to_all x1, starting transfers between devices, per_device(): lax.all_to_all(out_slip.reshape(slab_count, capacity, 3, marker_width), '...  14.3 us
    all_to_all x1, waiting for transfers between devices, per_device(): lax.all_to_all(reply_rows.reshape(slab_count, capacity, 3, marker_width),...  12.3 us
    all_to_all x1, waiting for transfers between devices, per_device(): lax.all_to_all(out_slip.reshape(slab_count, capacity, 3, marker_width), '...  11.6 us
    ppermute x2, starting transfers between devices, extended(): lax.ppermute(lax.slice_in_dim(block, 0, width, axis=dim), axis, backward)  11.4 us
    dot_general x8, matrix products, spread_block(): lax.dot_general(row_pick, placed, (((0,), (0,)), ((), ())), preferred_ele...  8.27 us
  transfers between devices with their start and end apart: 7, of which 5 were waited for; matrix products, arithmetic and copies ran while one was open for 29% of the time, Pallas kernels for 0%

commit v1 on v0

v1 whole, which is shorter than its diff:
```python
import functools

import jax
import jax.numpy as jnp
from jax import lax
from jax.experimental import pallas as pl
from jax.experimental.pallas import tpu as pltpu
from jax.sharding import PartitionSpec as P

DIRS = [
    (0, 0, 0),
    (1, 0, 0),
    (-1, 0, 0),
    (0, 1, 0),
    (0, -1, 0),
    (0, 0, 1),
    (0, 0, -1),
    (1, 1, 0),
    (-1, -1, 0),
    (1, -1, 0),
    (-1, 1, 0),
    (1, 0, 1),
    (-1, 0, -1),
    (1, 0, -1),
    (-1, 0, 1),
    (0, 1, 1),
    (0, -1, -1),
    (0, 1, -1),
    (0, -1, 1),
]
WEIGHTS = [1.0 / 3.0] + [1.0 / 18.0] * 6 + [1.0 / 36.0] * 12
OPPOSITE = [0, 2, 1, 4, 3, 6, 5, 8, 7, 10, 9, 12, 11, 14, 13, 16, 15, 18, 17]
OMEGA = 1.25
X_UP = [i for i in range(19) if DIRS[i][0] == 1]
X_DOWN = [i for i in range(19) if DIRS[i][0] == -1]
Y_UP = [i for i in range(19) if DIRS[i][1] == 1]
Y_DOWN = [i for i in range(19) if DIRS[i][1] == -1]

F32 = jnp.float32
BF16 = jnp.bfloat16
NN = (((1,), (0,)), ((), ()))
NT = (((1,), (1,)), ((), ()))
TN = (((0,), (0,)), ((), ()))


def dot(a, b, dims=NN):
    return lax.dot_general(a, b, dims, preferred_element_type=F32)


def iota(shape, axis):
    return lax.broadcasted_iota(jnp.int32, shape, axis)


def ones_at(mask):
    return jnp.where(mask, 1.0, 0.0).astype(BF16)


def split_two(value):
    high = value.astype(BF16)
    return high, (value - high.astype(F32)).astype(BF16)


def moments(pops_ref):
    pops = [pops_ref[i] for i in range(19)]
    density = functools.reduce(lambda a, b: a + b, pops)
    moment = []
    for c in range(3):
        up = functools.reduce(lambda a, b: a + b, [pops[i] for i in range(19) if DIRS[i][c] == 1])
        down = functools.reduce(lambda a, b: a + b, [pops[i] for i in range(19) if DIRS[i][c] == -1])
        moment.append(up - down)
    return density, moment


def flow_table(pops_ref, flow_ref):
    rows = pops_ref.shape[1]
    density, moment = moments(pops_ref)
    for c in range(3):
        flow_ref[pl.ds(c * rows, rows), :] = moment[c] / density


def slot_columns(velocity_ref, mcount_ref, pcount_ref, cols_ref):
    slots = mcount_ref.shape[1]
    lim = jnp.where(iota((1, slots), 1) < pcount_ref[...], mcount_ref[...], 0).astype(F32)
    stack = [velocity_ref[...].reshape(3, slots)] if velocity_ref is not None else [jnp.zeros((3, slots), F32)]
    stack = jnp.concatenate(stack + [lim, jnp.zeros((4, slots), F32)], axis=0)
    cols_ref[...] = stack.T


def routes(pid_ref, table_ref, pcount_ref, width):
    slots, slabs = pid_ref.shape[1], table_ref.shape[1]
    ids = pid_ref[...]
    alive = iota((1, slots), 1) < pcount_ref[...]
    in_range = ones_at(iota((slabs, slots), 0) == ids // slots)
    owner_of = ones_at(iota((slabs, slabs), 0) == table_ref[...])
    owner = jnp.where(alive, dot(owner_of, in_range), 0.0)
    before = ones_at(iota((slots, slots), 0) < iota((slots, slots), 1))
    earlier = dot(owner.astype(BF16), before)
    first = jnp.where(earlier < 0.5, owner, 0.0)
    pick = jnp.concatenate([first, owner - first], axis=0).astype(BF16)
    spot = (ids % slots + 1).astype(F32)
    spots = dot(pick, jnp.broadcast_to(spot, (width, slots)).astype(BF16), NT)
    return pick, spots


def sample(cell_ref, flow_ref, cols_ref, slip_ref):
    slots, width = cell_ref.shape
    rows = flow_ref.shape[0] // 3
    depth = flow_ref.shape[1]

    def block(g, carry):
        at = pl.multiple_of(g * 8, 8)
        cell = cell_ref[pl.ds(at, 8), :]
        z = cell % depth
        y = cell // depth
        picked = [jnp.zeros((8, width), F32) for _ in range(3)]
        for row in range(rows):
            here = y == row
            for c in range(3):
                line = jnp.broadcast_to(flow_ref[c * rows + row : c * rows + row + 1, :], (8, depth))
                got = jnp.take_along_axis(line, z, axis=1, mode="promise_in_bounds")
                picked[c] = jnp.where(here, got, picked[c])
        cols = cols_ref[pl.ds(at, 8), :]
        live = iota((8, width), 1).astype(F32) < cols[:, 3:4]
        for c in range(3):
            slip_ref[c, pl.ds(at, 8), :] = jnp.where(live, cols[:, c : c + 1] - picked[c], 0.0)
        return carry

    lax.fori_loop(0, slots // 8, block, 0)


def put_rows(wide_ref, rows, width):
    slabs = wide_ref.shape[0] // 8
    for p in range(2):
        for c in range(3):
            wide_ref[pl.ds(p * 3 + c, slabs, stride=8), :] = rows[
                p * slabs : (p + 1) * slabs, c * width : (c + 1) * width
            ]


def take_rows(wide_ref):
    slabs = wide_ref.shape[0] // 8
    sides = []
    for p in range(2):
        sides.append(
            jnp.concatenate(
                [wide_ref[pl.ds(p * 3 + c, slabs, stride=8), :] for c in range(3)], axis=1
            )
        )
    return jnp.concatenate(sides, axis=0).astype(BF16)


def front_kernel(
    pops_ref, cell_ref, mcount_ref, pcount_ref, pid_ref, table_ref, velocity_ref,
    message_ref, pick_ref, flow_ref, cols_ref, slip_ref, wide_ref,
):
    slots, width = cell_ref.shape
    slabs = slots // 2
    pick, spots = routes(pid_ref, table_ref, pcount_ref, width)
    pick_ref[...] = pick
    flow_table(pops_ref, flow_ref)
    slot_columns(velocity_ref, mcount_ref, pcount_ref, cols_ref)
    sample(cell_ref, flow_ref, cols_ref, slip_ref)
    slip = jnp.concatenate([slip_ref[c].astype(BF16) for c in range(3)], axis=1)
    put_rows(wide_ref, dot(pick_ref[...], slip), width)
    for p in range(2):
        wide_ref[pl.ds(6 + p, slabs, stride=8), :] = spots[p * slabs : (p + 1) * slabs]
    message_ref[...] = wide_ref[...].reshape(slabs, 8, width).astype(BF16)


def owner_kernel(
    got_ref, partner_ref, gap_ref, self_ref, pair_ref, reply_ref, wide_ref,
):
    slabs, _, width = got_ref.shape
    slots = 2 * slabs
    wide_ref[...] = got_ref[...].astype(F32).reshape(8 * slabs, width)
    owned = take_rows(wide_ref)
    spot_col = jnp.concatenate(
        [wide_ref[pl.ds(6 + p, slabs, stride=8), :] for p in range(2)], axis=0
    )
    head = ones_at(iota((slots, width), 1) == 0)
    spot_row = dot(head, spot_col.astype(BF16), NT)
    pairs = jnp.concatenate([partner_ref[...].astype(F32), gap_ref[...]], axis=0).T
    weight = jnp.zeros((slots, slots), F32)
    for k in range(4):
        weight += jnp.where(pairs[:, k : k + 1] + 1.0 == spot_row, 1.0 / pairs[:, 4 + k : 5 + k], 0.0)
    high, low = split_two(weight)
    near = (dot(high, owned) + dot(low, owned)).astype(BF16)
    place = jnp.where(spot_col[:, :1] - 1.0 == iota((slots, slots), 1).astype(F32), 1.0, 0.0).astype(BF16)
    near = dot(place, near).astype(BF16)
    parts = []
    for c in range(3):
        side = slice(c * width, (c + 1) * width)
        parts.append(dot(owned[:, side], self_ref[...]) + dot(near[:, side], pair_ref[...]))
    put_rows(wide_ref, jnp.concatenate(parts, axis=1), width)
    reply_ref[...] = wide_ref[...].reshape(slabs, 8, width).astype(BF16)


def spread(cell_ref, force_ref, rows, depth):
    slots, width = cell_ref.shape
    high_iota = iota((16, width), 0).astype(F32).astype(BF16)

    def block(g, total):
        at = pl.multiple_of(g * 8, 8)
        cell = cell_ref[pl.ds(at, 8), :]
        zf = (cell % depth).astype(F32)
        yf = (cell // depth).astype(F32)
        vals = [force_ref[c, pl.ds(at, 8), :] for c in range(3)]

        def packed(value, j):
            return jnp.broadcast_to(value[j : j + 1, :], (16, width)).astype(BF16)

        for pair in range(4):
            a_side, b_side = [], []
            for j in (2 * pair, 2 * pair + 1):
                zb, yb = packed(zf, j), packed(yf, j)
                one, zero = jnp.ones((16, width), BF16), jnp.zeros((16, width), BF16)
                b_side.append(
                    jnp.concatenate(
                        [jnp.where(zb == high_iota + 16 * i, one, zero) for i in range(depth // 16)], axis=0
                    )
                )
                marks = [yb == high_iota + 16 * i for i in range(rows // 16)]
                lines = []
                for c in range(3):
                    vb = packed(vals[c], j)
                    lines += [jnp.where(mark, vb, zero) for mark in marks]
                a_side.append(jnp.concatenate(lines, axis=0))
            total = total + dot(jnp.concatenate(a_side, axis=1), jnp.concatenate(b_side, axis=1), NT)
        return total

    return lax.fori_loop(0, slots // 8, block, jnp.zeros((3 * rows, depth), F32))


def collide(pops_ref, force, out_ref):
    density, moment = moments(pops_ref)
    inverse = 1.0 / density
    velocity = [(moment[c] + 0.5 * force[c]) * inverse for c in range(3)]
    speed_sq = velocity[0] * velocity[0] + velocity[1] * velocity[1] + velocity[2] * velocity[2]
    work = velocity[0] * force[0] + velocity[1] * force[1] + velocity[2] * force[2]

    def along(i, parts):
        terms = [parts[c] if DIRS[i][c] == 1 else -parts[c] for c in range(3) if DIRS[i][c] != 0]
        return functools.reduce(lambda a, b: a + b, terms) if terms else None

    for i in range(19):
        w = WEIGHTS[i]
        cu, cf = along(i, velocity), along(i, force)
        base = 1.0 - 1.5 * speed_sq
        if cu is None:
            equilibrium = w * density * base
            source = (1.0 - 0.5 * OMEGA) * w * (-3.0 * work)
        else:
            equilibrium = w * density * (base + 3.0 * cu + 4.5 * cu * cu)
            source = (1.0 - 0.5 * OMEGA) * w * (3.0 * (cf - work) + 9.0 * cu * cf)
        pops = pops_ref[i]
        out_ref[i] = pops - OMEGA * (pops - equilibrium) + source


def back_kernel(
    returned_ref, pick_ref, pops_ref, cell_ref, mcount_ref, pcount_ref,
    marker_ref, collided_ref, cols_ref, force_ref, wide_ref,
):
    slots, width = cell_ref.shape
    slabs = slots // 2
    rows, depth = pops_ref.shape[1:]
    wide_ref[...] = returned_ref[...].astype(F32).reshape(8 * slabs, width)
    own = dot(pick_ref[...], take_rows(wide_ref), TN)
    slot_columns(None, mcount_ref, pcount_ref, cols_ref)
    live = iota((slots, width), 1).astype(F32) < cols_ref[:, 3:4]
    for c in range(3):
        value = jnp.where(live, own[:, c * width : (c + 1) * width], 0.0)
        force_ref[c] = value
        marker_ref[c] = value.astype(BF16)
    total = spread(cell_ref, force_ref, rows, depth)
    collide(pops_ref, [total[c * rows : (c + 1) * rows] for c in range(3)], collided_ref)


def stream(collided_ref, x_low_ref, x_high_ref, y_low_ref, y_high_ref, read_ref, sub_total):
    rows, depth = collided_ref.shape[1:]
    me = lax.axis_index("sub")
    row = iota((rows, depth), 0)
    for i in range(19):
        sx, sy, sz = DIRS[i]
        if sx == 0:
            value = collided_ref[i]
        elif sx == 1:
            value = x_low_ref[X_UP.index(i)]
        else:
            value = x_high_ref[X_DOWN.index(i)]
        if sy == 1:
            edge = y_low_ref[Y_UP.index(i)]
            value = jnp.where(row == 0, edge[0:1, :], pltpu.roll(value, 1, 0))
        elif sy == -1:
            edge = y_high_ref[Y_DOWN.index(i)]
            value = jnp.where(row == rows - 1, edge[0:1, :], pltpu.roll(value, rows - 1, 0))
        if sz != 0:
            value = pltpu.roll(value, sz % depth, 1)
        if sy != 0:
            wall_row, wall_device = (0, 0) if sy == 1 else (rows - 1, sub_total - 1)
            at_wall = (row == wall_row) & (me == wall_device)
            value = jnp.where(at_wall, collided_ref[OPPOSITE[i]], value)
        read_ref[i] = value


def vmem(n):
    return [pl.BlockSpec(memory_space=pltpu.VMEM)] * n


def call(body, outs, scratch, args, name):
    return pl.pallas_call(
        body,
        out_shape=[jax.ShapeDtypeStruct(shape, kind) for shape, kind in outs],
        in_specs=vmem(len(args)),
        out_specs=vmem(len(outs)),
        scratch_shapes=[pltpu.VMEM(shape, kind) for shape, kind in scratch],
        name=name,
    )(*args)


def per_device(
    populations, marker_cell, marker_count, particle_count, particle_id, owner_table,
    particle_velocity, pair_list, pair_gap, self_coupling, pair_coupling,
):
    rows, depth = populations.shape[2:]
    slots, width = marker_cell.shape[2:]
    slabs = lax.axis_size("slab")
    pops = populations[:, 0]
    cell = marker_cell[0, 0]
    mcount = marker_count[0]
    pid = particle_id[0]
    velocity = jnp.transpose(particle_velocity[0], (1, 0, 2))
    partners = jnp.transpose(pair_list[0, 0])
    gaps = jnp.transpose(pair_gap[0, 0])
    message, pick = call(
        front_kernel,
        [((slabs, 8, width), BF16), ((slots, slots), BF16)],
        [((3 * rows, depth), F32), ((slots, 8), F32), ((3, slots, width), F32), ((8 * slabs, width), F32)],
        (pops, cell, mcount, particle_count, pid, owner_table, velocity),
        "front",
    )
    got = lax.all_to_all(message, "slab", split_axis=0, concat_axis=0, tiled=True)
    (reply,) = call(
        owner_kernel,
        [((slabs, 8, width), BF16)],
        [((8 * slabs, width), F32)],
        (got, partners, gaps, self_coupling, pair_coupling),
        "owner",
    )
    returned = lax.all_to_all(reply, "slab", split_axis=0, concat_axis=0, tiled=True)
    marker, collided = call(
        back_kernel,
        [((3, slots, width), BF16), ((19, rows, depth), F32)],
        [((slots, 8), F32), ((3, slots, width), F32), ((8 * slabs, width), F32)],
        (returned, pick, pops, cell, mcount, particle_count),
        "back",
    )
    up = [(i, (i + 1) % slabs) for i in range(slabs)]
    down = [(b, a) for a, b in up]
    x_low = lax.ppermute(jnp.stack([collided[i] for i in X_UP]), "slab", up)
    x_high = lax.ppermute(jnp.stack([collided[i] for i in X_DOWN]), "slab", down)

    def plane(i):
        return {0: collided, 1: x_low, -1: x_high}[DIRS[i][0]][
            {0: i, 1: X_UP.index(i) if i in X_UP else 0, -1: X_DOWN.index(i) if i in X_DOWN else 0}[DIRS[i][0]]
        ]

    subs = lax.axis_size("sub")
    forward = [(i, i + 1) for i in range(subs - 1)]
    y_low = lax.ppermute(jnp.stack([plane(i)[rows - 1 :] for i in Y_UP]), "sub", forward)
    y_high = lax.ppermute(jnp.stack([plane(i)[:1] for i in Y_DOWN]), "sub", [(b, a) for a, b in forward])
    (read,) = call(
        functools.partial(stream, sub_total=subs),
        [((19, rows, depth), F32)],
        [],
        (collided, x_low, x_high, y_low, y_high),
        "stream",
    )
    return read[:, None], jnp.transpose(marker, (1, 0, 2))[None, None]


def solution(mesh):
    placed = (
        P(None, "slab", "sub", None),
        P("slab", "sub", None, None),
        P("slab", "sub", None),
        P("slab", "sub"),
        P("slab", "sub", None),
        P("sub", None),
        P("slab", "sub", None, None),
        P("slab", "sub", None, None),
        P("slab", "sub", None, None),
        P(),
        P(),
    )
    return jax.shard_map(
        per_device,
        mesh=mesh,
        in_specs=placed,
        out_specs=(P(None, "slab", "sub", None), P("slab", "sub", None, None, None)),
        check_vma=False,
    )
```

time: 200 us -> 106 us (0.53); the launches traced: 197 us -> 105 us
  blocking collectives: 0 us -> 54.4 us
  starting transfers between devices: 53 us -> 8.31 us
  local copies, waits for them, and re-layouts: 51 us -> 6.4 us
  matrix products: 34.5 us -> 0 us
  other arithmetic: 28 us -> 0 us
  Pallas kernels: 0 us -> 23.3 us
  waiting for transfers between devices: 27.7 us -> 11.1 us
    all_to_all x0 -> x2, blocking collectives: none -> 54.4 us  [the longest x1 32.6 us: per_device(): lax.all_to_all(message, 'slab', split_axis=0, concat_axis=0, tiled=True)]
    all_to_all x3 -> x0, starting transfers between devices: 38.2 us -> none  [the longest x1 17.8 us: per_device(): lax.all_to_all(out_spot.reshape(slab_count, capacity), 'slab', split_axis...]
    dot_general x21 -> x0, matrix products: 34.5 us -> none  [the longest x8 21.3 us: sample_block(): jnp.dot(row_pick, flow_field, precision=lax.Precision.HIGHEST, preferred_...]
    all_to_all x3 -> x0, waiting for transfers between devices: 24 us -> none  [the longest x1 12.3 us: per_device(): lax.all_to_all(reply_rows.reshape(slab_count, capacity, 3, marker_width),...]
    pallas_call x0 -> x4, Pallas kernels: none -> 23.3 us  [call(): pl.pallas_call(body, out_shape=[jax.ShapeDtypeStruct(shape, kind) for sha...]
    scatter x3 -> x0, local copies, waits for them, and re-layouts: 15.7 us -> none  [the longest x1 7.32 us: per_device(): owned = jnp.zeros((slot_count, 3, marker_width), jnp.bfloat16).at[landing...]
    dynamic_slice x16 -> x0, local copies, waits for them, and re-layouts: 14.8 us -> none  [sample_markers(): lax.map(sample_block, flat_cells.reshape(-1, block_size)).reshape(-1, 3)]
    reduce_sum x13 -> x0, other arithmetic: 10.7 us -> none  [the longest x8 6.05 us: sample_block(): return jnp.sum(jnp.where(depth_pick[:, None, :], picked_rows, 0.0), axis=2)]
  transfers between devices with their start and end apart: 7 -> 4, of which waited for: 5 -> 2; matrix products, arithmetic and copies ran while one was open for 29% -> 1% of each run, Pallas kernels for 0% -> 0%
where the time goes in v1:
time: 106 us; the launch traced here: 105 us
  blocking collectives  54.4 us (51%)
  Pallas kernels  23.3 us (22%)
  waiting for transfers between devices  11.1 us (10%)
  starting transfers between devices  8.31 us (8%)
  local copies, waits for them, and re-layouts  6.4 us (6%)
  between operations  1.37 us (1%)
    all_to_all x1, blocking collectives, per_device(): lax.all_to_all(message, 'slab', split_axis=0, concat_axis=0, tiled=True)  32.6 us
    pallas_call x4, Pallas kernels, call(): pl.pallas_call(body, out_shape=[jax.ShapeDtypeStruct(shape, kind) for sha...  23.3 us
    all_to_all x1, blocking collectives, per_device(): lax.all_to_all(reply, 'slab', split_axis=0, concat_axis=0, tiled=True)  21.8 us
    ppermute x1, waiting for transfers between devices, per_device(): x_low = lax.ppermute(jnp.stack([collided[i] for i in X_UP]), 'slab', up)  6.91 us
    unnamed x17, local copies, waits for them, and re-layouts  4.98 us
    ppermute x1, waiting for transfers between devices, per_device(): lax.ppermute(jnp.stack([plane(i)[rows - 1:] for i in Y_UP]), 'sub', forward)  4.16 us
    ppermute x1, starting transfers between devices, per_device(): lax.ppermute(jnp.stack([plane(i)[:1] for i in Y_DOWN]), 'sub', [(b, a) fo...  2.72 us
    ppermute x1, starting transfers between devices, per_device(): lax.ppermute(jnp.stack([collided[i] for i in X_DOWN]), 'slab', down)  2.18 us
  transfers between devices with their start and end apart: 4, of which 2 were waited for; matrix products, arithmetic and copies ran while one was open for 1% of the time, Pallas kernels for 0%

profile of v1, /device:TPU:6, one launch (start us, length us, event | category | flops | bytes accessed | tf_op | source)
XLA Modules:
  0.0 104.9 jit_solution(3158715919174393083)
XLA Ops:
  1.3 8.5 %front.1 = (bf16[128,8,128]{2,1,0:T(8,128)(2,1)}, bf16[256,256]{1,0:T(8,128)(2,1)}) custom-call(f32[19,32,128]{2,1,0:T(8,128)} %bitcast.17, s32[256,128]{1,0:T(8,128)} %bitcast.19, s32[1,256]{1,0:T(1,128)} %bitcast.24, s32[1,1]{1,0:T(1,128)S(6)} %copy.30.pcount_ref, s32[1,256]{1,0:T(1,128)} %bitcast.27, s32[1,128]{1,0:T(1,128)} %table_ref.1, ...), custom_call_target="tpu_custom_call" | custom-call | tf_op jit(solution)/shard_map/front/pallas_call | solution.py:310
  9.7 32.6 %all_to_all.10.got_ref = bf16[128,8,128]{2,1,0:T(8,128)(2,1)} all-to-all(bf16[128,8,128]{2,1,0:T(8,128)(2,1)} %get-tuple-element.6), channel_id=1, replica_groups=mesh['slab'=128,'sub'=4] {'slab'}, dimensions={0} | all-to-all | bytes 524288 | tf_op jit(solution)/shard_map/all_to_all | solution.py:341
  42.3 3.0 %owner.1 = bf16[128,8,128]{2,1,0:T(8,128)(2,1)} custom-call(bf16[128,8,128]{2,1,0:T(8,128)(2,1)} %all_to_all.10.got_ref, s32[4,256]{1,0:T(4,128)} %bitcast.22, f32[4,256]{1,0:T(4,128)} %bitcast.23, bf16[128,128]{1,0:T(8,128)(2,1)} %self_ref.1, bf16[128,128]{1,0:T(8,128)(2,1)} %pair_ref.1), custom_call_target="tpu_custom_call" | custom-call | tf_op jit(solution)/shard_map/owner/pallas_call | solution.py:310
  45.3 21.8 %all_to_all.11.returned_ref = bf16[128,8,128]{2,1,0:T(8,128)(2,1)} all-to-all(bf16[128,8,128]{2,1,0:T(8,128)(2,1)} %owner.1), channel_id=1, replica_groups=mesh['slab'=128,'sub'=4] {'slab'}, dimensions={0} | all-to-all | bytes 524288 | tf_op jit(solution)/shard_map/all_to_all | solution.py:349
  67.1 10.0 %back.1 = (bf16[3,256,128]{2,1,0:T(8,128)(2,1)}, f32[19,32,128]{2,1,0:T(8,128)}) custom-call(bf16[128,8,128]{2,1,0:T(8,128)(2,1)} %all_to_all.11.returned_ref, bf16[256,256]{1,0:T(8,128)(2,1)} %get-tuple-element.7.pick_ref, f32[19,32,128]{2,1,0:T(8,128)} %bitcast.18, s32[256,128]{1,0:T(8,128)} %bitcast.20, s32[1,256]{1,0:T(1,128)} %bitcast.25, ...), custom_call_target="tpu_custom_call" | custom-call | tf_op jit(solution)/shard_map/back/pallas_call | solution.py:310
  77.1 0.7 constant_dynamic-update-slice_fusion.9
  77.9 0.7 constant_dynamic-update-slice_fusion.8
  78.6 0.7 constant_dynamic-update-slice_fusion.7
  79.4 0.7 constant_dynamic-update-slice_fusion.6
  80.1 0.7 constant_dynamic-update-slice_fusion.5
  80.8 2.2 %collective-permute-start.1 = (f32[5,32,128]{2,1,0:T(8,128)S(1)}, f32[5,32,128]{2,1,0:T(8,128)S(1)}, u32[]{:S(2)}, u32[]{:S(2)}) collective-permute-start(f32[5,32,128]{2,1,0:T(8,128)S(1)} %get-tuple-element.18), channel_id=1, source_target_pairs={{4,0},{8,4},{12,8},{16,12},{20,16},{24,20},{28,24},{32,28},{36,32}... | collective-permute-start | bytes 245768 | tf_op jit(solution)/shard_map/ppermute | solution.py:360
  83.0 0.7 constant_dynamic-update-slice_fusion.19
  83.7 2.1 %collective-permute-start = (f32[5,32,128]{2,1,0:T(8,128)S(1)}, f32[5,32,128]{2,1,0:T(8,128)S(1)}, u32[]{:S(2)}, u32[]{:S(2)}) collective-permute-start(f32[5,32,128]{2,1,0:T(8,128)S(1)} %get-tuple-element.19), channel_id=1, source_target_pairs={{0,4},{4,8},{8,12},{12,16},{16,20},{20,24},{24,28},{28,32},{32,36}... | collective-permute-start | bytes 245768 | tf_op jit(solution)/shard_map/ppermute | solution.py:359
  85.8 0.0 collective-permute-done.1.x_high_ref
  85.9 0.0 copy-start.1
  85.9 6.9 %collective-permute-done.x_low_ref = f32[5,32,128]{2,1,0:T(8,128)S(1)} collective-permute-done((f32[5,32,128]{2,1,0:T(8,128)S(1)}, f32[5,32,128]{2,1,0:T(8,128)S(1)}, u32[]{:S(2)}, u32[]{:S(2)}) %collective-permute-start) | collective-permute-done | bytes 81952 | tf_op jit(solution)/shard_map/ppermute | solution.py:359
  92.8 0.0 copy-start
  92.8 0.7 constant_dynamic-update-slice_fusion.16
  93.5 0.7 constant_dynamic-update-slice_fusion.15
  94.2 2.7 %collective-permute-start.3 = (f32[5,1,128]{2,1,0:T(1,128)S(1)}, f32[5,1,128]{2,1,0:T(1,128)S(1)}, u32[]{:S(2)}, u32[]{:S(2)}) collective-permute-start(f32[5,1,128]{2,1,0:T(1,128)S(1)} %get-tuple-element.12), channel_id=1, source_target_pairs={{1,0},{2,1},{3,2},{5,4},{6,5},{7,6},{9,8},{10,9},{11,10},{13,12},{... | collective-permute-start | bytes 7688 | tf_op jit(solution)/shard_map/ppermute | solution.py:370
  96.9 1.3 %collective-permute-start.2 = (f32[5,1,128]{2,1,0:T(1,128)S(1)}, f32[5,1,128]{2,1,0:T(1,128)S(1)}, u32[]{:S(2)}, u32[]{:S(2)}) collective-permute-start(f32[5,1,128]{2,1,0:T(1,128)S(1)} %get-tuple-element.13), channel_id=1, source_target_pairs={{0,1},{1,2},{2,3},{4,5},{5,6},{6,7},{8,9},{9,10},{10,11},{12,13},{... | collective-permute-start | bytes 7688 | tf_op jit(solution)/shard_map/ppermute | solution.py:369
  98.2 0.0 collective-permute-done.3.y_high_ref
  98.2 0.0 copy-start.2
  98.3 4.2 %collective-permute-done.2.y_low_ref = f32[5,1,128]{2,1,0:T(1,128)S(1)} collective-permute-done((f32[5,1,128]{2,1,0:T(1,128)S(1)}, f32[5,1,128]{2,1,0:T(1,128)S(1)}, u32[]{:S(2)}, u32[]{:S(2)}) %collective-permute-start.2) | collective-permute-done | bytes 2592 | tf_op jit(solution)/shard_map/ppermute | solution.py:369
  102.4 0.0 copy-done.1
  102.4 0.0 copy-done
  102.4 0.0 copy-done.2
  102.4 0.0 copy-start.3
  102.4 0.6 copy-done.3
  103.0 1.9 %stream.1 = f32[19,32,128]{2,1,0:T(8,128)} custom-call(f32[19,32,128]{2,1,0:T(8,128)} %get-tuple-element.8.collided_ref, f32[5,32,128]{2,1,0:T(8,128)} %copy-done, f32[5,32,128]{2,1,0:T(8,128)} %copy-done.1, f32[5,1,128]{2,1,0:T(1,128)} %copy-done.3, f32[5,1,128]{2,1,0:T(1,128)} %copy-done.2), custom_call_target="tpu_custom_call" | custom-call | tf_op jit(solution)/shard_map/stream/pallas_call | solution.py:310
  (3 shorter events, 0.0 us)
Async XLA Ops:
  80.8 5.0 %collective-permute-start.1 = (f32[5,32,128]{2,1,0:T(8,128)S(1)}, f32[5,32,128]{2,1,0:T(8,128)S(1)}, u32[]{:S(2)}, u32[]{:S(2)}) collective-permute-start(f32[5,32,128]{2,1,0:T(8,128)S(1)} %get-tuple-element.18), channel_id=1, source_target_pairs={{4,0},{8,4},{12,8},{16,12},{20,16},{24,20},{28,24},{32,28},{36,32}... | collective-permute-start | bytes 245768 | tf_op jit(solution)/shard_map/ppermute | solution.py:360
  83.7 9.1 %collective-permute-start = (f32[5,32,128]{2,1,0:T(8,128)S(1)}, f32[5,32,128]{2,1,0:T(8,128)S(1)}, u32[]{:S(2)}, u32[]{:S(2)}) collective-permute-start(f32[5,32,128]{2,1,0:T(8,128)S(1)} %get-tuple-element.19), channel_id=1, source_target_pairs={{0,4},{4,8},{8,12},{12,16},{16,20},{20,24},{24,28},{28,32},{32,36}... | collective-permute-start | bytes 245768 | tf_op jit(solution)/shard_map/ppermute | solution.py:359
  85.9 16.6 %copy-start.1 = (f32[5,32,128]{2,1,0:T(8,128)}, f32[5,32,128]{2,1,0:T(8,128)S(1)}, u32[]{:S(2)}) copy-start(f32[5,32,128]{2,1,0:T(8,128)S(1)} %collective-permute-done.1.x_high_ref) | copy-start | bytes 245764
  92.8 9.6 %copy-start = (f32[5,32,128]{2,1,0:T(8,128)}, f32[5,32,128]{2,1,0:T(8,128)S(1)}, u32[]{:S(2)}) copy-start(f32[5,32,128]{2,1,0:T(8,128)S(1)} %collective-permute-done.x_low_ref) | copy-start | bytes 245764
  94.2 4.0 %collective-permute-start.3 = (f32[5,1,128]{2,1,0:T(1,128)S(1)}, f32[5,1,128]{2,1,0:T(1,128)S(1)}, u32[]{:S(2)}, u32[]{:S(2)}) collective-permute-start(f32[5,1,128]{2,1,0:T(1,128)S(1)} %get-tuple-element.12), channel_id=1, source_target_pairs={{1,0},{2,1},{3,2},{5,4},{6,5},{7,6},{9,8},{10,9},{11,10},{13,12},{... | collective-permute-start | bytes 7688 | tf_op jit(solution)/shard_map/ppermute | solution.py:370
  96.9 5.5 %collective-permute-start.2 = (f32[5,1,128]{2,1,0:T(1,128)S(1)}, f32[5,1,128]{2,1,0:T(1,128)S(1)}, u32[]{:S(2)}, u32[]{:S(2)}) collective-permute-start(f32[5,1,128]{2,1,0:T(1,128)S(1)} %get-tuple-element.13), channel_id=1, source_target_pairs={{0,1},{1,2},{2,3},{4,5},{5,6},{6,7},{8,9},{9,10},{10,11},{12,13},{... | collective-permute-start | bytes 7688 | tf_op jit(solution)/shard_map/ppermute | solution.py:369
  98.2 4.2 %copy-start.2 = (f32[5,1,128]{2,1,0:T(1,128)}, f32[5,1,128]{2,1,0:T(1,128)S(1)}, u32[]{:S(2)}) copy-start(f32[5,1,128]{2,1,0:T(1,128)S(1)} %collective-permute-done.3.y_high_ref) | copy-start | bytes 7684
  102.4 0.6 copy-start.3

commit v2 on v1

--- a/solution.py
+++ b/solution.py
@@ -55,6 +55,10 @@
     return jnp.where(mask, 1.0, 0.0).astype(BF16)
 
 
+def split_cell(cell, depth):
+    return cell & (depth - 1), lax.shift_right_logical(cell, depth.bit_length() - 1)
+
+
 def split_two(value):
     high = value.astype(BF16)
     return high, (value - high.astype(F32)).astype(BF16)
@@ -110,8 +114,7 @@
     def block(g, carry):
         at = pl.multiple_of(g * 8, 8)
         cell = cell_ref[pl.ds(at, 8), :]
-        z = cell % depth
-        y = cell // depth
+        z, y = split_cell(cell, depth)
         picked = [jnp.zeros((8, width), F32) for _ in range(3)]
         for row in range(rows):
             here = y == row
@@ -149,12 +152,100 @@
     return jnp.concatenate(sides, axis=0).astype(BF16)
 
 
-def front_kernel(
-    pops_ref, cell_ref, mcount_ref, pcount_ref, pid_ref, table_ref, velocity_ref,
-    message_ref, pick_ref, flow_ref, cols_ref, slip_ref, wide_ref,
-):
-    slots, width = cell_ref.shape
-    slabs = slots // 2
+ORDER = X_UP + X_DOWN + [3, 4, 15, 16, 17, 18, 0, 5, 6]
+PLACE = [ORDER.index(i) for i in range(19)]
+EDGES = [3, 15, 17, 7, 10, 4, 16, 18, 9, 8]
+
+
+def routed(mesh_ids):
+    return dict(device_id=mesh_ids, device_id_type=pl.DeviceIdType.MESH)
+
+
+def near_ids():
+    slabs, subs = lax.axis_size("slab"), lax.axis_size("sub")
+    me, side = lax.axis_index("slab"), lax.axis_index("sub")
+    next_slab, last_slab = lax.rem(me + 1, slabs), lax.rem(me + slabs - 1, slabs)
+    next_sub, last_sub = lax.rem(side + 1, subs), lax.rem(side + subs - 1, subs)
+    return [
+        {"slab": me, "sub": next_sub},
+        {"slab": next_slab, "sub": next_sub},
+        {"slab": last_slab, "sub": next_sub},
+        {"slab": me, "sub": last_sub},
+        {"slab": next_slab, "sub": last_sub},
+        {"slab": last_slab, "sub": last_sub},
+        {"slab": next_slab, "sub": side},
+        {"slab": last_slab, "sub": side},
+    ]
+
+
+def greet():
+    slabs = lax.axis_size("slab")
+    me, side = lax.axis_index("slab"), lax.axis_index("sub")
+    barrier = pltpu.get_barrier_semaphore()
+
+    def one(k, carry):
+        pl.semaphore_signal(barrier, inc=1, **routed({"slab": lax.rem(me + k, slabs), "sub": side}))
+        return carry
+
+    lax.fori_loop(1, slabs, one, 0)
+    for ids in near_ids()[:6]:
+        pl.semaphore_signal(barrier, inc=1, **routed(ids))
+
+
+def met():
+    pl.semaphore_wait(pltpu.get_barrier_semaphore(), lax.axis_size("slab") + 5)
+
+
+def exchange_start(out_ref, in_ref, send_sem, recv_sem, own_sem):
+    slabs = lax.axis_size("slab")
+    me, side = lax.axis_index("slab"), lax.axis_index("sub")
+
+    def one(k, carry):
+        to = lax.rem(me + k, slabs)
+        pltpu.make_async_remote_copy(
+            src_ref=out_ref.at[to],
+            dst_ref=in_ref.at[me],
+            send_sem=send_sem,
+            recv_sem=recv_sem,
+            **routed({"slab": to, "sub": side}),
+        ).start()
+        return carry
+
+    lax.fori_loop(1, slabs, one, 0)
+    pltpu.make_async_copy(out_ref.at[me], in_ref.at[me], own_sem).start()
+
+
+def exchange_wait(out_ref, in_ref, send_sem, recv_sem, own_sem):
+    slabs = lax.axis_size("slab")
+    me = lax.axis_index("slab")
+    others = pl.ds(0, slabs - 1)
+    pltpu.make_async_copy(out_ref.at[me], in_ref.at[me], own_sem).wait()
+    pltpu.make_async_copy(in_ref.at[others], in_ref.at[others], recv_sem).wait()
+    pltpu.make_async_copy(out_ref.at[others], out_ref.at[others], send_sem).wait()
+
+
+def halo_copies(collided_ref, x_low_ref, x_high_ref, edge_out_ref, edge_in_ref, send_sem, recv_sem):
+    ids = near_ids()
+    views = [(edge_out_ref.at[pl.ds(a, n)], edge_in_ref.at[pl.ds(a, n)]) for a, n in ((0, 3), (3, 1), (4, 1), (5, 3), (8, 1), (9, 1))]
+    views.append((collided_ref.at[pl.ds(0, 5)], x_low_ref))
+    views.append((collided_ref.at[pl.ds(5, 5)], x_high_ref))
+    return [
+        pltpu.make_async_remote_copy(
+            src_ref=source,
+            dst_ref=target,
+            send_sem=send_sem.at[n],
+            recv_sem=recv_sem.at[n],
+            **routed(ids[n]),
+        )
+        for n, (source, target) in enumerate(views)
+    ]
+
+
+def send_slip(refs):
+    (cell_ref, mcount_ref, pcount_ref, pid_ref, table_ref, velocity_ref, pops_ref,
+     flow_ref, cols_ref, slip_ref, wide_ref, pick_ref, message_ref) = refs
+    width = cell_ref.shape[1]
+    slabs = message_ref.shape[0]
     pick, spots = routes(pid_ref, table_ref, pcount_ref, width)
     pick_ref[...] = pick
     flow_table(pops_ref, flow_ref)
@@ -167,9 +258,7 @@
     message_ref[...] = wide_ref[...].reshape(slabs, 8, width).astype(BF16)
 
 
-def owner_kernel(
-    got_ref, partner_ref, gap_ref, self_ref, pair_ref, reply_ref, wide_ref,
-):
+def lubricate(got_ref, partner_ref, gap_ref, self_ref, pair_ref, reply_ref, wide_ref):
     slabs, _, width = got_ref.shape
     slots = 2 * slabs
     wide_ref[...] = got_ref[...].astype(F32).reshape(8 * slabs, width)
@@ -185,7 +274,7 @@
         weight += jnp.where(pairs[:, k : k + 1] + 1.0 == spot_row, 1.0 / pairs[:, 4 + k : 5 + k], 0.0)
     high, low = split_two(weight)
     near = (dot(high, owned) + dot(low, owned)).astype(BF16)
-    place = jnp.where(spot_col[:, :1] - 1.0 == iota((slots, slots), 1).astype(F32), 1.0, 0.0).astype(BF16)
+    place = ones_at(spot_col[:, :1] - 1.0 == iota((slots, slots), 1).astype(F32))
     near = dot(place, near).astype(BF16)
     parts = []
     for c in range(3):
@@ -202,8 +291,7 @@
     def block(g, total):
         at = pl.multiple_of(g * 8, 8)
         cell = cell_ref[pl.ds(at, 8), :]
-        zf = (cell % depth).astype(F32)
-        yf = (cell // depth).astype(F32)
+        zf, yf = (part.astype(F32) for part in split_cell(cell, depth))
         vals = [force_ref[c, pl.ds(at, 8), :] for c in range(3)]
 
         def packed(value, j):
@@ -231,21 +319,21 @@
     return lax.fori_loop(0, slots // 8, block, jnp.zeros((3 * rows, depth), F32))
 
 
-def collide(pops_ref, force, out_ref):
+def along(i, parts):
+    terms = [parts[c] if DIRS[i][c] == 1 else -parts[c] for c in range(3) if DIRS[i][c] != 0]
+    return functools.reduce(lambda a, b: a + b, terms) if terms else None
+
+
+def collide(pops_ref, force, out_ref, chosen):
     density, moment = moments(pops_ref)
     inverse = 1.0 / density
     velocity = [(moment[c] + 0.5 * force[c]) * inverse for c in range(3)]
     speed_sq = velocity[0] * velocity[0] + velocity[1] * velocity[1] + velocity[2] * velocity[2]
     work = velocity[0] * force[0] + velocity[1] * force[1] + velocity[2] * force[2]
-
-    def along(i, parts):
-        terms = [parts[c] if DIRS[i][c] == 1 else -parts[c] for c in range(3) if DIRS[i][c] != 0]
-        return functools.reduce(lambda a, b: a + b, terms) if terms else None
-
-    for i in range(19):
+    base = 1.0 - 1.5 * speed_sq
+    for i in chosen:
         w = WEIGHTS[i]
         cu, cf = along(i, velocity), along(i, force)
-        base = 1.0 - 1.5 * speed_sq
         if cu is None:
             equilibrium = w * density * base
             source = (1.0 - 0.5 * OMEGA) * w * (-3.0 * work)
@@ -253,68 +341,78 @@
             equilibrium = w * density * (base + 3.0 * cu + 4.5 * cu * cu)
             source = (1.0 - 0.5 * OMEGA) * w * (3.0 * (cf - work) + 9.0 * cu * cf)
         pops = pops_ref[i]
-        out_ref[i] = pops - OMEGA * (pops - equilibrium) + source
-
-
-def back_kernel(
-    returned_ref, pick_ref, pops_ref, cell_ref, mcount_ref, pcount_ref,
-    marker_ref, collided_ref, cols_ref, force_ref, wide_ref,
-):
-    slots, width = cell_ref.shape
-    slabs = slots // 2
-    rows, depth = pops_ref.shape[1:]
-    wide_ref[...] = returned_ref[...].astype(F32).reshape(8 * slabs, width)
-    own = dot(pick_ref[...], take_rows(wide_ref), TN)
-    slot_columns(None, mcount_ref, pcount_ref, cols_ref)
-    live = iota((slots, width), 1).astype(F32) < cols_ref[:, 3:4]
-    for c in range(3):
-        value = jnp.where(live, own[:, c * width : (c + 1) * width], 0.0)
-        force_ref[c] = value
-        marker_ref[c] = value.astype(BF16)
-    total = spread(cell_ref, force_ref, rows, depth)
-    collide(pops_ref, [total[c * rows : (c + 1) * rows] for c in range(3)], collided_ref)
-
-
-def stream(collided_ref, x_low_ref, x_high_ref, y_low_ref, y_high_ref, read_ref, sub_total):
+        out_ref[PLACE[i]] = pops - OMEGA * (pops - equilibrium) + source
+
+
+def stream(chosen, collided_ref, x_low_ref, x_high_ref, edge_ref, read_ref):
     rows, depth = collided_ref.shape[1:]
     me = lax.axis_index("sub")
+    last = lax.axis_size("sub") - 1
     row = iota((rows, depth), 0)
-    for i in range(19):
+    for i in chosen:
         sx, sy, sz = DIRS[i]
         if sx == 0:
-            value = collided_ref[i]
+            value = collided_ref[PLACE[i]]
         elif sx == 1:
             value = x_low_ref[X_UP.index(i)]
         else:
             value = x_high_ref[X_DOWN.index(i)]
         if sy == 1:
-            edge = y_low_ref[Y_UP.index(i)]
-            value = jnp.where(row == 0, edge[0:1, :], pltpu.roll(value, 1, 0))
+            value = jnp.where(row == 0, edge_ref[EDGES.index(i)], pltpu.roll(value, 1, 0))
         elif sy == -1:
-            edge = y_high_ref[Y_DOWN.index(i)]
-            value = jnp.where(row == rows - 1, edge[0:1, :], pltpu.roll(value, rows - 1, 0))
+            value = jnp.where(row == rows - 1, edge_ref[EDGES.index(i)], pltpu.roll(value, rows - 1, 0))
         if sz != 0:
             value = pltpu.roll(value, sz % depth, 1)
         if sy != 0:
-            wall_row, wall_device = (0, 0) if sy == 1 else (rows - 1, sub_total - 1)
+            wall_row, wall_device = (0, 0) if sy == 1 else (rows - 1, last)
             at_wall = (row == wall_row) & (me == wall_device)
-            value = jnp.where(at_wall, collided_ref[OPPOSITE[i]], value)
+            value = jnp.where(at_wall, collided_ref[PLACE[OPPOSITE[i]]], value)
         read_ref[i] = value
 
 
-def vmem(n):
-    return [pl.BlockSpec(memory_space=pltpu.VMEM)] * n
-
-
-def call(body, outs, scratch, args, name):
-    return pl.pallas_call(
-        body,
-        out_shape=[jax.ShapeDtypeStruct(shape, kind) for shape, kind in outs],
-        in_specs=vmem(len(args)),
-        out_specs=vmem(len(outs)),
-        scratch_shapes=[pltpu.VMEM(shape, kind) for shape, kind in scratch],
-        name=name,
-    )(*args)
+def step_kernel(
+    pops_ref, cell_ref, mcount_ref, pcount_ref, pid_ref, table_ref, velocity_ref,
+    partner_ref, gap_ref, self_ref, pair_ref,
+    read_ref, marker_ref,
+    flow_ref, cols_ref, slip_ref, wide_ref, pick_ref, message_ref, got_ref, reply_ref, returned_ref,
+    collided_ref, x_low_ref, x_high_ref, edge_out_ref, edge_in_ref,
+    bulk_sem, own_sem, halo_send, halo_recv,
+):
+    slots, width = cell_ref.shape
+    rows, depth = pops_ref.shape[1:]
+    greet()
+    send_slip((cell_ref, mcount_ref, pcount_ref, pid_ref, table_ref, velocity_ref, pops_ref,
+               flow_ref, cols_ref, slip_ref, wide_ref, pick_ref, message_ref))
+    met()
+    there = (message_ref, got_ref, bulk_sem.at[0], bulk_sem.at[1], own_sem.at[0])
+    exchange_start(*there)
+    exchange_wait(*there)
+    lubricate(got_ref, partner_ref, gap_ref, self_ref, pair_ref, reply_ref, wide_ref)
+    back = (reply_ref, returned_ref, bulk_sem.at[2], bulk_sem.at[3], own_sem.at[1])
+    exchange_start(*back)
+    exchange_wait(*back)
+    wide_ref[...] = returned_ref[...].astype(F32).reshape(wide_ref.shape)
+    own = dot(pick_ref[...], take_rows(wide_ref), TN)
+    live = iota((slots, width), 1).astype(F32) < cols_ref[:, 3:4]
+    for c in range(3):
+        value = jnp.where(live, own[:, c * width : (c + 1) * width], 0.0)
+        slip_ref[c] = value
+        marker_ref[c] = value.astype(BF16)
+    total = spread(cell_ref, slip_ref, rows, depth)
+    force = [total[c * rows : (c + 1) * rows] for c in range(3)]
+    collide(pops_ref, force, collided_ref, ORDER)
+    for n, i in enumerate(EDGES):
+        at = rows - 1 if DIRS[i][1] == 1 else 0
+        edge_out_ref[n] = collided_ref[PLACE[i], at : at + 1, :]
+    copies = halo_copies(collided_ref, x_low_ref, x_high_ref, edge_out_ref, edge_in_ref, halo_send, halo_recv)
+    for copy in copies:
+        copy.start()
+    streams = (collided_ref, x_low_ref, x_high_ref, edge_in_ref, read_ref)
+    inner = [0, 5, 6]
+    stream(inner, *streams)
+    for copy in copies:
+        copy.wait()
+    stream([i for i in range(19) if i not in inner], *streams)
 
 
 def per_device(
@@ -324,57 +422,55 @@
     rows, depth = populations.shape[2:]
     slots, width = marker_cell.shape[2:]
     slabs = lax.axis_size("slab")
-    pops = populations[:, 0]
-    cell = marker_cell[0, 0]
-    mcount = marker_count[0]
-    pid = particle_id[0]
-    velocity = jnp.transpose(particle_velocity[0], (1, 0, 2))
-    partners = jnp.transpose(pair_list[0, 0])
-    gaps = jnp.transpose(pair_gap[0, 0])
-    message, pick = call(
-        front_kernel,
-        [((slabs, 8, width), BF16), ((slots, slots), BF16)],
-        [((3 * rows, depth), F32), ((slots, 8), F32), ((3, slots, width), F32), ((8 * slabs, width), F32)],
-        (pops, cell, mcount, particle_count, pid, owner_table, velocity),
-        "front",
+    args = (
+        populations[:, 0],
+        marker_cell[0, 0],
+        marker_count[0],
+        particle_count,
+        particle_id[0],
+        owner_table,
+        jnp.transpose(particle_velocity[0], (1, 0, 2)),
+        jnp.transpose(pair_list[0, 0]),
+        jnp.transpose(pair_gap[0, 0]),
+        self_coupling,
+        pair_coupling,
     )
-    got = lax.all_to_all(message, "slab", split_axis=0, concat_axis=0, tiled=True)
-    (reply,) = call(
-        owner_kernel,
-        [((slabs, 8, width), BF16)],
-        [((8 * slabs, width), F32)],
-        (got, partners, gaps, self_coupling, pair_coupling),
-        "owner",
-    )
-    returned = lax.all_to_all(reply, "slab", split_axis=0, concat_axis=0, tiled=True)
-    marker, collided = call(
-        back_kernel,
-        [((3, slots, width), BF16), ((19, rows, depth), F32)],
-        [((slots, 8), F32), ((3, slots, width), F32), ((8 * slabs, width), F32)],
-        (returned, pick, pops, cell, mcount, particle_count),
-        "back",
-    )
-    up = [(i, (i + 1) % slabs) for i in range(slabs)]
-    down = [(b, a) for a, b in up]
-    x_low = lax.ppermute(jnp.stack([collided[i] for i in X_UP]), "slab", up)
-    x_high = lax.ppermute(jnp.stack([collided[i] for i in X_DOWN]), "slab", down)
-
-    def plane(i):
-        return {0: collided, 1: x_low, -1: x_high}[DIRS[i][0]][
-            {0: i, 1: X_UP.index(i) if i in X_UP else 0, -1: X_DOWN.index(i) if i in X_DOWN else 0}[DIRS[i][0]]
-        ]
-
-    subs = lax.axis_size("sub")
-    forward = [(i, i + 1) for i in range(subs - 1)]
-    y_low = lax.ppermute(jnp.stack([plane(i)[rows - 1 :] for i in Y_UP]), "sub", forward)
-    y_high = lax.ppermute(jnp.stack([plane(i)[:1] for i in Y_DOWN]), "sub", [(b, a) for a, b in forward])
-    (read,) = call(
-        functools.partial(stream, sub_total=subs),
-        [((19, rows, depth), F32)],
-        [],
-        (collided, x_low, x_high, y_low, y_high),
-        "stream",
-    )
+    place = pl.BlockSpec(memory_space=pltpu.VMEM)
+    post = ((slabs, 8, width), BF16)
+    scratch = [
+        ((3 * rows, depth), F32),
+        ((slots, 8), F32),
+        ((3, slots, width), F32),
+        ((8 * slabs, width), F32),
+        ((slots, slots), BF16),
+        post,
+        post,
+        post,
+        post,
+        ((19, rows, depth), F32),
+        ((5, rows, depth), F32),
+        ((5, rows, depth), F32),
+        ((10, 1, depth), F32),
+        ((10, 1, depth), F32),
+    ]
+    read, marker = pl.pallas_call(
+        step_kernel,
+        out_shape=[
+            jax.ShapeDtypeStruct((19, rows, depth), F32),
+            jax.ShapeDtypeStruct((3, slots, width), BF16),
+        ],
+        in_specs=[place] * len(args),
+        out_specs=[place] * 2,
+        scratch_shapes=[pltpu.VMEM(shape, kind) for shape, kind in scratch]
+        + [
+            pltpu.SemaphoreType.DMA((4,)),
+            pltpu.SemaphoreType.DMA((2,)),
+            pltpu.SemaphoreType.DMA((8,)),
+            pltpu.SemaphoreType.DMA((8,)),
+        ],
+        compiler_params=pltpu.CompilerParams(collective_id=0, has_side_effects=True),
+        name="step",
+    )(*args)
     return read[:, None], jnp.transpose(marker, (1, 0, 2))[None, None]
 
 

time: 106 us -> 59.2 us (0.56)
  blocking collectives: 54.4 us -> 0 us
  Pallas kernels: 23.3 us -> 54.7 us
  waiting for transfers between devices: 11.1 us -> 0 us
  starting transfers between devices: 8.31 us -> 0 us
  local copies, waits for them, and re-layouts: 6.4 us -> 2.43 us
    all_to_all x2 -> x0, blocking collectives: 54.4 us -> none  [the longest x1 32.6 us: per_device(): lax.all_to_all(message, 'slab', split_axis=0, concat_axis=0, tiled=True)]
    pallas_call x4 -> x1, Pallas kernels: 23.3 us -> 54.7 us  [per_device(): pl.pallas_call(step_kernel, out_shape=[jax.ShapeDtypeStruct((19, rows, de...]
    ppermute x4 -> x0, waiting for transfers between devices: 11.1 us -> none  [the longest x1 6.91 us: per_device(): x_low = lax.ppermute(jnp.stack([collided[i] for i in X_UP]), 'slab', up)]
    ppermute x4 -> x0, starting transfers between devices: 8.31 us -> none  [the longest x1 2.72 us: per_device(): lax.ppermute(jnp.stack([plane(i)[:1] for i in Y_DOWN]), 'sub', [(b, a) fo...]
    unnamed x17 -> x4, local copies, waits for them, and re-layouts: 4.98 us -> 2.43 us
    another operation x2 -> x0, local copies, waits for them, and re-layouts: 1.42 us -> none  [the longest x1 0.74 us: per_device(): jnp.stack([collided[i] for i in X_DOWN])]
  transfers between devices with their start and end apart: 4 -> 0, of which waited for: 2 -> 0; matrix products, arithmetic and copies ran while one was open for 1% -> 0% of each run, Pallas kernels for 0% -> 0%
where the time goes in v2:
time: 59.2 us; the launch traced here: 58.4 us
  Pallas kernels  54.7 us (92%)
  local copies, waits for them, and re-layouts  2.43 us (4%)
  between operations  1.3 us (2%)
    pallas_call x1, Pallas kernels, per_device(): pl.pallas_call(step_kernel, out_shape=[jax.ShapeDtypeStruct((19, rows, de...  54.7 us
    unnamed x4, local copies, waits for them, and re-layouts  2.43 us

profile of v2, /device:TPU:6, one launch (start us, length us, event | category | flops | bytes accessed | tf_op | source)
XLA Modules:
  0.0 58.4 jit_solution(4410490060286625080)
XLA Ops:
  1.3 54.7 %step.1 = (f32[19,32,128]{2,1,0:T(8,128)}, bf16[3,256,128]{2,1,0:T(8,128)(2,1)}) custom-call(f32[19,32,128]{2,1,0:T(8,128)} %bitcast.18, s32[256,128]{1,0:T(8,128)} %bitcast.20, s32[1,256]{1,0:T(1,128)} %bitcast.24, s32[1,1]{1,0:T(1,128)S(6)} %copy.16.pcount_ref, s32[1,256]{1,0:T(1,128)} %bitcast.25, s32[1,128]{1,0:T(1,128)} %table_ref.1, ...), custom_call_target="tpu_custom_call" | custom-call | tf_op jit(solution)/shard_map/step/pallas_call | solution.py:456
  56.0 0.0 copy-start
  56.0 1.7 %copy.17 = f32[19,1,32,128]{3,2,1,0:T(8,128)} copy(f32[19,1,32,128]{3,2,1,0:T(8,128)} %bitcast.17) | data formatting | bytes 622592
  57.8 0.0 copy-done
  57.8 0.7 %copy.18 = bf16[1,1,256,3,128]{4,2,3,1,0:T(8,128)(2,1)} copy(bf16[1,1,256,3,128]{4,2,3,1,0:T(8,128)(2,1)S(1)} %bitcast.19) | data formatting | bytes 393216
Async XLA Ops:
  56.0 1.8 %copy-start = (bf16[3,256,128]{2,1,0:T(8,128)(2,1)S(1)}, bf16[3,256,128]{2,1,0:T(8,128)(2,1)}, u32[]{:S(2)}) copy-start(bf16[3,256,128]{2,1,0:T(8,128)(2,1)} %get-tuple-element.5) | copy-start | bytes 589828

commit v3 on v2

--- a/solution.py
+++ b/solution.py
@@ -31,6 +31,10 @@
 WEIGHTS = [1.0 / 3.0] + [1.0 / 18.0] * 6 + [1.0 / 36.0] * 12
 OPPOSITE = [0, 2, 1, 4, 3, 6, 5, 8, 7, 10, 9, 12, 11, 14, 13, 16, 15, 18, 17]
 OMEGA = 1.25
+SAMPLE_GROUP = 8
+SPREAD_GROUP = 16
+FIXED = float(1 << 21)
+VMEM_LIMIT = 60 * 1024 * 1024
 X_UP = [i for i in range(19) if DIRS[i][0] == 1]
 X_DOWN = [i for i in range(19) if DIRS[i][0] == -1]
 Y_UP = [i for i in range(19) if DIRS[i][1] == 1]
@@ -78,8 +82,17 @@
 def flow_table(pops_ref, flow_ref):
     rows = pops_ref.shape[1]
     density, moment = moments(pops_ref)
-    for c in range(3):
-        flow_ref[pl.ds(c * rows, rows), :] = moment[c] / density
+    x, y, z = ((moment[c] / density * FIXED + 0.5 * FIXED + 0.5).astype(jnp.int32) for c in range(3))
+    high = lax.shift_right_logical(z, 10)
+    flow_ref[pl.ds(0, rows), :] = lax.shift_left(x, 11) + high
+    flow_ref[pl.ds(rows, rows), :] = lax.shift_left(y, 11) + (z & 1023)
+
+
+def unpack_flow(first, second):
+    x = lax.shift_right_logical(first, 11)
+    y = lax.shift_right_logical(second, 11)
+    z = lax.shift_left(first & 2047, 10) + (second & 2047)
+    return [value.astype(F32) * (1.0 / FIXED) - 0.5 for value in (x, y, z)]
 
 
 def slot_columns(velocity_ref, mcount_ref, pcount_ref, cols_ref):
@@ -106,29 +119,33 @@
     return pick, spots
 
 
-def sample(cell_ref, flow_ref, cols_ref, slip_ref):
+def sample(cell_ref, flow_ref, cols_ref, slip_ref, half):
     slots, width = cell_ref.shape
-    rows = flow_ref.shape[0] // 3
+    rows = flow_ref.shape[0] // 2
     depth = flow_ref.shape[1]
+    group = min(SAMPLE_GROUP, slots // 8)
 
     def block(g, carry):
-        at = pl.multiple_of(g * 8, 8)
-        cell = cell_ref[pl.ds(at, 8), :]
-        z, y = split_cell(cell, depth)
-        picked = [jnp.zeros((8, width), F32) for _ in range(3)]
-        for row in range(rows):
-            here = y == row
+        for n in range(group):
+            at = pl.multiple_of(g * 8 * group + 8 * n, 8)
+            z, y = split_cell(cell_ref[pl.ds(at, 8), :], depth)
+            picked = [jnp.zeros((8, width), jnp.int32) for _ in range(2)]
+            for row in range(rows):
+                here = y == row
+                for c in range(2):
+                    line = jnp.broadcast_to(flow_ref[c * rows + row : c * rows + row + 1, :], (8, depth))
+                    got = jnp.take_along_axis(line, z, axis=1, mode="promise_in_bounds")
+                    picked[c] = jnp.where(here, got, picked[c])
+            cols = cols_ref[pl.ds(at, 8), :]
+            flow = unpack_flow(*picked)
+            live = iota((8, width), 1).astype(F32) < cols[:, 3:4]
             for c in range(3):
-                line = jnp.broadcast_to(flow_ref[c * rows + row : c * rows + row + 1, :], (8, depth))
-                got = jnp.take_along_axis(line, z, axis=1, mode="promise_in_bounds")
-                picked[c] = jnp.where(here, got, picked[c])
-        cols = cols_ref[pl.ds(at, 8), :]
-        live = iota((8, width), 1).astype(F32) < cols[:, 3:4]
-        for c in range(3):
-            slip_ref[c, pl.ds(at, 8), :] = jnp.where(live, cols[:, c : c + 1] - picked[c], 0.0)
+                slip_ref[c, pl.ds(at, 8), :] = jnp.where(live, cols[:, c : c + 1] - flow[c], 0.0)
         return carry
 
-    lax.fori_loop(0, slots // 8, block, 0)
+    steps = slots // (8 * group)
+    middle = steps // 2
+    lax.fori_loop(middle if half else 0, steps if half else middle, block, 0)
 
 
 def put_rows(wide_ref, rows, width):
@@ -178,50 +195,86 @@
     ]
 
 
+def inner_size():
+    return 16 if lax.axis_size("slab") % 32 == 0 else 4
+
+
 def greet():
-    slabs = lax.axis_size("slab")
-    me, side = lax.axis_index("slab"), lax.axis_index("sub")
+    side = lax.axis_index("sub")
     barrier = pltpu.get_barrier_semaphore()
-
-    def one(k, carry):
-        pl.semaphore_signal(barrier, inc=1, **routed({"slab": lax.rem(me + k, slabs), "sub": side}))
-        return carry
-
-    lax.fori_loop(1, slabs, one, 0)
+    for to in row_peers() + column_peers():
+        pl.semaphore_signal(barrier, inc=1, **routed({"slab": to, "sub": side}))
     for ids in near_ids()[:6]:
         pl.semaphore_signal(barrier, inc=1, **routed(ids))
 
 
-def met():
-    pl.semaphore_wait(pltpu.get_barrier_semaphore(), lax.axis_size("slab") + 5)
-
-
-def exchange_start(out_ref, in_ref, send_sem, recv_sem, own_sem):
-    slabs = lax.axis_size("slab")
+def row_peers():
+    inner, me = inner_size(), lax.axis_index("slab")
+    base = me // inner * inner
+    return [base + lax.rem(me + k, inner) for k in range(1, inner)]
+
+
+def column_peers():
+    slabs, inner, me = lax.axis_size("slab"), inner_size(), lax.axis_index("slab")
+    return [lax.rem(me + k * inner, slabs) for k in range(1, slabs // inner)]
+
+
+def relay(row_sem):
+    side = lax.axis_index("sub")
+    rows, columns = row_peers(), column_peers()
+    pl.semaphore_wait(pltpu.get_barrier_semaphore(), len(rows) + len(columns) + 6)
+    for to in columns:
+        pl.semaphore_signal(row_sem, inc=1, **routed({"slab": to, "sub": side}))
+
+
+def met(row_sem):
+    pl.semaphore_wait(row_sem, len(column_peers()))
+
+
+def far_first(size):
+    return sorted(range(size), key=lambda step: -min(step, size - step))
+
+
+def exchange_start(out_ref, in_ref, send_sem, recv_sem, own_sem, lines):
+    slabs, inner = lax.axis_size("slab"), inner_size()
+    outer, ring = slabs // inner, inner // 2
     me, side = lax.axis_index("slab"), lax.axis_index("sub")
-
-    def one(k, carry):
-        to = lax.rem(me + k, slabs)
+    bases = [lax.rem(me // inner + step, outer) * inner for step in far_first(outer)]
+    place = lax.rem(me, inner) // 2
+    cores = [lax.rem(me + 1, 2), lax.rem(me, 2)]
+
+    def send(to):
         pltpu.make_async_remote_copy(
-            src_ref=out_ref.at[to],
-            dst_ref=in_ref.at[me],
+            src_ref=out_ref.at[to, pl.ds(0, lines)],
+            dst_ref=in_ref.at[me, pl.ds(0, lines)],
             send_sem=send_sem,
             recv_sem=recv_sem,
             **routed({"slab": to, "sub": side}),
         ).start()
+
+    def one(j, carry):
+        step = ring // 2 + (j + 1) // 2 * (1 - 2 * lax.rem(j + 1, 2))
+        here = lax.rem(place + step, ring) * 2
+        for base in bases:
+            for core in cores:
+                send(base + here + core)
         return carry
 
-    lax.fori_loop(1, slabs, one, 0)
+    lax.fori_loop(0, ring - 1, one, 0)
+    for base in bases[:-1]:
+        for core in cores:
+            send(base + place * 2 + core)
+    send(bases[-1] + place * 2 + cores[0])
     pltpu.make_async_copy(out_ref.at[me], in_ref.at[me], own_sem).start()
 
 
-def exchange_wait(out_ref, in_ref, send_sem, recv_sem, own_sem):
+def exchange_wait(out_ref, in_ref, send_sem, recv_sem, own_sem, lines):
     slabs = lax.axis_size("slab")
     me = lax.axis_index("slab")
     others = pl.ds(0, slabs - 1)
     pltpu.make_async_copy(out_ref.at[me], in_ref.at[me], own_sem).wait()
-    pltpu.make_async_copy(in_ref.at[others], in_ref.at[others], recv_sem).wait()
-    pltpu.make_async_copy(out_ref.at[others], out_ref.at[others], send_sem).wait()
+    pltpu.make_async_copy(in_ref.at[others, pl.ds(0, lines)], in_ref.at[others, pl.ds(0, lines)], recv_sem).wait()
+    pltpu.make_async_copy(out_ref.at[others, pl.ds(0, lines)], out_ref.at[others, pl.ds(0, lines)], send_sem).wait()
 
 
 def halo_copies(collided_ref, x_low_ref, x_high_ref, edge_out_ref, edge_in_ref, send_sem, recv_sem):
@@ -241,24 +294,40 @@
     ]
 
 
+def scope(name):
+    return jax.named_scope(name)
+
+
 def send_slip(refs):
     (cell_ref, mcount_ref, pcount_ref, pid_ref, table_ref, velocity_ref, pops_ref,
-     flow_ref, cols_ref, slip_ref, wide_ref, pick_ref, message_ref) = refs
+     flow_ref, cols_ref, slip_ref, wide_ref, pick_ref, message_ref, row_sem) = refs
     width = cell_ref.shape[1]
     slabs = message_ref.shape[0]
-    pick, spots = routes(pid_ref, table_ref, pcount_ref, width)
-    pick_ref[...] = pick
-    flow_table(pops_ref, flow_ref)
-    slot_columns(velocity_ref, mcount_ref, pcount_ref, cols_ref)
-    sample(cell_ref, flow_ref, cols_ref, slip_ref)
+    with scope("q1_routes"):
+        pick, spots = routes(pid_ref, table_ref, pcount_ref, width)
+        pick_ref[...] = pick
+        for p in range(2):
+            wide_ref[pl.ds(6 + p, slabs, stride=8), :] = spots[p * slabs : (p + 1) * slabs]
+    with scope("q2_flow"):
+        flow_table(pops_ref, flow_ref)
+    with scope("q3_cols"):
+        slot_columns(velocity_ref, mcount_ref, pcount_ref, cols_ref)
+    with scope("q4_sample"):
+        sample(cell_ref, flow_ref, cols_ref, slip_ref, 0)
+    with scope("q5_relay"):
+        relay(row_sem)
+    with scope("q6_sample"):
+        sample(cell_ref, flow_ref, cols_ref, slip_ref, 1)
     slip = jnp.concatenate([slip_ref[c].astype(BF16) for c in range(3)], axis=1)
     put_rows(wide_ref, dot(pick_ref[...], slip), width)
-    for p in range(2):
-        wide_ref[pl.ds(6 + p, slabs, stride=8), :] = spots[p * slabs : (p + 1) * slabs]
     message_ref[...] = wide_ref[...].reshape(slabs, 8, width).astype(BF16)
 
 
-def lubricate(got_ref, partner_ref, gap_ref, self_ref, pair_ref, reply_ref, wide_ref):
+def pair_columns(partner_ref, gap_ref, pairs_ref):
+    pairs_ref[...] = jnp.concatenate([partner_ref[...].astype(F32) + 1.0, 1.0 / gap_ref[...]], axis=0).T
+
+
+def lubricate(got_ref, pairs_ref, self_ref, pair_ref, reply_ref, wide_ref):
     slabs, _, width = got_ref.shape
     slots = 2 * slabs
     wide_ref[...] = got_ref[...].astype(F32).reshape(8 * slabs, width)
@@ -268,10 +337,10 @@
     )
     head = ones_at(iota((slots, width), 1) == 0)
     spot_row = dot(head, spot_col.astype(BF16), NT)
-    pairs = jnp.concatenate([partner_ref[...].astype(F32), gap_ref[...]], axis=0).T
+    pairs = pairs_ref[...]
     weight = jnp.zeros((slots, slots), F32)
     for k in range(4):
-        weight += jnp.where(pairs[:, k : k + 1] + 1.0 == spot_row, 1.0 / pairs[:, 4 + k : 5 + k], 0.0)
+        weight += jnp.where(pairs[:, k : k + 1] == spot_row, pairs[:, 4 + k : 5 + k], 0.0)
     high, low = split_two(weight)
     near = (dot(high, owned) + dot(low, owned)).astype(BF16)
     place = ones_at(spot_col[:, :1] - 1.0 == iota((slots, slots), 1).astype(F32))
@@ -284,39 +353,53 @@
     reply_ref[...] = wide_ref[...].reshape(slabs, 8, width).astype(BF16)
 
 
-def spread(cell_ref, force_ref, rows, depth):
+def packed_row(value, j):
+    return jnp.broadcast_to(value[j : j + 1, :], (16, value.shape[1])).astype(BF16)
+
+
+def mark_depths(cell_ref, hot_ref, depth):
     slots, width = cell_ref.shape
-    high_iota = iota((16, width), 0).astype(F32).astype(BF16)
+    lines = iota((16, width), 0).astype(F32).astype(BF16)
+    one, zero = jnp.ones((16, width), BF16), jnp.zeros((16, width), BF16)
+
+    def block(g, carry):
+        z = split_cell(cell_ref[pl.ds(pl.multiple_of(g * 8, 8), 8), :], depth)[0].astype(F32)
+        for j in range(8):
+            zb = packed_row(z, j)
+            for i in range(depth // 16):
+                hot_ref[g, 16 * i : 16 * (i + 1), j * width : (j + 1) * width] = jnp.where(
+                    zb == lines + 16 * i, one, zero
+                )
+        return carry
+
+    lax.fori_loop(0, slots // 8, block, 0)
+
+
+def spread(cell_ref, force_ref, hot_ref, rows, depth):
+    slots, width = cell_ref.shape
+    lines = iota((16, width), 0).astype(F32).astype(BF16)
+    zero = jnp.zeros((16, width), BF16)
+
+    group = min(SPREAD_GROUP, slots // 8)
 
     def block(g, total):
-        at = pl.multiple_of(g * 8, 8)
-        cell = cell_ref[pl.ds(at, 8), :]
-        zf, yf = (part.astype(F32) for part in split_cell(cell, depth))
-        vals = [force_ref[c, pl.ds(at, 8), :] for c in range(3)]
-
-        def packed(value, j):
-            return jnp.broadcast_to(value[j : j + 1, :], (16, width)).astype(BF16)
-
-        for pair in range(4):
-            a_side, b_side = [], []
-            for j in (2 * pair, 2 * pair + 1):
-                zb, yb = packed(zf, j), packed(yf, j)
-                one, zero = jnp.ones((16, width), BF16), jnp.zeros((16, width), BF16)
-                b_side.append(
-                    jnp.concatenate(
-                        [jnp.where(zb == high_iota + 16 * i, one, zero) for i in range(depth // 16)], axis=0
-                    )
-                )
-                marks = [yb == high_iota + 16 * i for i in range(rows // 16)]
-                lines = []
+        for n in range(group):
+            at = pl.multiple_of(g * 8 * group + 8 * n, 8)
+            y = split_cell(cell_ref[pl.ds(at, 8), :], depth)[1].astype(F32)
+            vals = [force_ref[c, pl.ds(at, 8), :] for c in range(3)]
+            sides = []
+            for j in range(8):
+                yb = packed_row(y, j)
+                marks = [yb == lines + 16 * i for i in range(rows // 16)]
+                stack = []
                 for c in range(3):
-                    vb = packed(vals[c], j)
-                    lines += [jnp.where(mark, vb, zero) for mark in marks]
-                a_side.append(jnp.concatenate(lines, axis=0))
-            total = total + dot(jnp.concatenate(a_side, axis=1), jnp.concatenate(b_side, axis=1), NT)
+                    vb = packed_row(vals[c], j)
+                    stack += [jnp.where(mark, vb, zero) for mark in marks]
+                sides.append(jnp.concatenate(stack, axis=0))
+            total = total + dot(jnp.concatenate(sides, axis=1), hot_ref[g * group + n], NT)
         return total
 
-    return lax.fori_loop(0, slots // 8, block, jnp.zeros((3 * rows, depth), F32))
+    return lax.fori_loop(0, slots // (8 * group), block, jnp.zeros((3 * rows, depth), F32))
 
 
 def along(i, parts):
@@ -370,49 +453,72 @@
         read_ref[i] = value
 
 
-def step_kernel(
-    pops_ref, cell_ref, mcount_ref, pcount_ref, pid_ref, table_ref, velocity_ref,
-    partner_ref, gap_ref, self_ref, pair_ref,
-    read_ref, marker_ref,
-    flow_ref, cols_ref, slip_ref, wide_ref, pick_ref, message_ref, got_ref, reply_ref, returned_ref,
-    collided_ref, x_low_ref, x_high_ref, edge_out_ref, edge_in_ref,
-    bulk_sem, own_sem, halo_send, halo_recv,
-):
+def step_kernel(*refs):
+    given, (read_ref, marker_ref), rest = refs[:11], refs[11:13], refs[13:]
+    held, rest = rest[:11], rest[11:]
+    (pops_ref, cell_ref, mcount_ref, pcount_ref, pid_ref, table_ref, velocity_ref,
+     partner_ref, gap_ref, self_ref, pair_ref) = held
+    (flow_ref, cols_ref, slip_ref, wide_ref, pick_ref, message_ref, got_ref, reply_ref, returned_ref,
+     collided_ref, x_low_ref, x_high_ref, edge_out_ref, edge_in_ref, hot_ref, pairs_ref,
+     load_sem, bulk_sem, own_sem, halo_send, halo_recv, row_sem) = rest
     slots, width = cell_ref.shape
     rows, depth = pops_ref.shape[1:]
-    greet()
-    send_slip((cell_ref, mcount_ref, pcount_ref, pid_ref, table_ref, velocity_ref, pops_ref,
-               flow_ref, cols_ref, slip_ref, wide_ref, pick_ref, message_ref))
-    met()
-    there = (message_ref, got_ref, bulk_sem.at[0], bulk_sem.at[1], own_sem.at[0])
-    exchange_start(*there)
-    exchange_wait(*there)
-    lubricate(got_ref, partner_ref, gap_ref, self_ref, pair_ref, reply_ref, wide_ref)
-    back = (reply_ref, returned_ref, bulk_sem.at[2], bulk_sem.at[3], own_sem.at[1])
-    exchange_start(*back)
-    exchange_wait(*back)
-    wide_ref[...] = returned_ref[...].astype(F32).reshape(wide_ref.shape)
-    own = dot(pick_ref[...], take_rows(wide_ref), TN)
-    live = iota((slots, width), 1).astype(F32) < cols_ref[:, 3:4]
-    for c in range(3):
-        value = jnp.where(live, own[:, c * width : (c + 1) * width], 0.0)
-        slip_ref[c] = value
-        marker_ref[c] = value.astype(BF16)
-    total = spread(cell_ref, slip_ref, rows, depth)
-    force = [total[c * rows : (c + 1) * rows] for c in range(3)]
-    collide(pops_ref, force, collided_ref, ORDER)
-    for n, i in enumerate(EDGES):
-        at = rows - 1 if DIRS[i][1] == 1 else 0
-        edge_out_ref[n] = collided_ref[PLACE[i], at : at + 1, :]
+    loads = [pltpu.make_async_copy(a, b, load_sem.at[n]) for n, (a, b) in enumerate(zip(given, held))]
+    for load in loads:
+        load.start()
+    with scope("p0_greet"):
+        greet()
+    with scope("p0_load"):
+        for load in loads:
+            load.wait()
+    with scope("p1_front"):
+        send_slip((cell_ref, mcount_ref, pcount_ref, pid_ref, table_ref, velocity_ref, pops_ref,
+                   flow_ref, cols_ref, slip_ref, wide_ref, pick_ref, message_ref, row_sem))
+    with scope("p2_met"):
+        met(row_sem)
+    there = (message_ref, got_ref, bulk_sem.at[0], bulk_sem.at[1], own_sem.at[0], 8)
+    with scope("p3_start"):
+        exchange_start(*there)
+    with scope("p3_mark"):
+        pair_columns(partner_ref, gap_ref, pairs_ref)
+        mark_depths(cell_ref, hot_ref, depth)
+    with scope("p4_wait"):
+        exchange_wait(*there)
+    with scope("p5_lub"):
+        lubricate(got_ref, pairs_ref, self_ref, pair_ref, reply_ref, wide_ref)
+    back = (reply_ref, returned_ref, bulk_sem.at[2], bulk_sem.at[3], own_sem.at[1], 6)
+    with scope("p6_start"):
+        exchange_start(*back)
+    with scope("p7_wait"):
+        exchange_wait(*back)
+    with scope("p8_unroute"):
+        wide_ref[...] = returned_ref[...].astype(F32).reshape(wide_ref.shape)
+        own = dot(pick_ref[...], take_rows(wide_ref), TN)
+        live = iota((slots, width), 1).astype(F32) < cols_ref[:, 3:4]
+        for c in range(3):
+            value = jnp.where(live, own[:, c * width : (c + 1) * width], 0.0)
+            slip_ref[c] = value
+            marker_ref[c] = value.astype(BF16)
+    with scope("p9_spread"):
+        total = spread(cell_ref, slip_ref, hot_ref, rows, depth)
+    with scope("pa_collide"):
+        force = [total[c * rows : (c + 1) * rows] for c in range(3)]
+        collide(pops_ref, force, collided_ref, ORDER)
+        for n, i in enumerate(EDGES):
+            at = rows - 1 if DIRS[i][1] == 1 else 0
+            edge_out_ref[n] = collided_ref[PLACE[i], at : at + 1, :]
     copies = halo_copies(collided_ref, x_low_ref, x_high_ref, edge_out_ref, edge_in_ref, halo_send, halo_recv)
     for copy in copies:
         copy.start()
     streams = (collided_ref, x_low_ref, x_high_ref, edge_in_ref, read_ref)
     inner = [0, 5, 6]
-    stream(inner, *streams)
-    for copy in copies:
-        copy.wait()
-    stream([i for i in range(19) if i not in inner], *streams)
+    with scope("pc_inner"):
+        stream(inner, *streams)
+    with scope("pd_hwait"):
+        for copy in copies:
+            copy.wait()
+    with scope("pe_stream"):
+        stream([i for i in range(19) if i not in inner], *streams)
 
 
 def per_device(
@@ -438,7 +544,7 @@
     place = pl.BlockSpec(memory_space=pltpu.VMEM)
     post = ((slabs, 8, width), BF16)
     scratch = [
-        ((3 * rows, depth), F32),
+        ((2 * rows, depth), jnp.int32),
         ((slots, 8), F32),
         ((3, slots, width), F32),
         ((8 * slabs, width), F32),
@@ -452,23 +558,30 @@
         ((5, rows, depth), F32),
         ((10, 1, depth), F32),
         ((10, 1, depth), F32),
+        ((slots // 8, depth, 8 * width), BF16),
+        ((slots, 8), F32),
     ]
+    held = [(arg.shape, arg.dtype) for arg in args]
     read, marker = pl.pallas_call(
         step_kernel,
         out_shape=[
             jax.ShapeDtypeStruct((19, rows, depth), F32),
             jax.ShapeDtypeStruct((3, slots, width), BF16),
         ],
-        in_specs=[place] * len(args),
+        in_specs=[pl.BlockSpec(memory_space=pltpu.HBM)] * len(args),
         out_specs=[place] * 2,
-        scratch_shapes=[pltpu.VMEM(shape, kind) for shape, kind in scratch]
+        scratch_shapes=[pltpu.VMEM(shape, kind) for shape, kind in held + scratch]
         + [
+            pltpu.SemaphoreType.DMA((len(args),)),
             pltpu.SemaphoreType.DMA((4,)),
             pltpu.SemaphoreType.DMA((2,)),
             pltpu.SemaphoreType.DMA((8,)),
             pltpu.SemaphoreType.DMA((8,)),
+            pltpu.SemaphoreType.REGULAR,
         ],
-        compiler_params=pltpu.CompilerParams(collective_id=0, has_side_effects=True),
+        compiler_params=pltpu.CompilerParams(
+            collective_id=0, has_side_effects=True, vmem_limit_bytes=VMEM_LIMIT
+        ),
         name="step",
     )(*args)
     return read[:, None], jnp.transpose(marker, (1, 0, 2))[None, None]

time: 59.2 us -> 49.8 us (0.84)
  the two profiles are of different devices: /device:TPU:6 before, /device:TPU:1 now
where the time goes in v3:
time: 49.8 us; the launch traced here: 49.6 us
  Pallas kernels  45.9 us (92%)
  local copies, waits for them, and re-layouts  2.43 us (5%)
  between operations  1.3 us (3%)
    pallas_call x1, Pallas kernels, per_device(): pl.pallas_call(step_kernel, out_shape=[jax.ShapeDtypeStruct((19, rows, de...  45.9 us
    unnamed x4, local copies, waits for them, and re-layouts  2.43 us

profile of v3, /device:TPU:1, one launch (start us, length us, event | category | flops | bytes accessed | tf_op | source)
XLA Modules:
  0.0 49.6 jit_solution(15312878061980126500)
XLA Ops:
  1.3 45.9 %step.1 = (f32[19,32,128]{2,1,0:T(8,128)}, bf16[3,256,128]{2,1,0:T(8,128)(2,1)}) custom-call(f32[19,32,128]{2,1,0:T(8,128)} %bitcast.18, s32[256,128]{1,0:T(8,128)} %bitcast.20, s32[1,256]{1,0:T(1,128)} %bitcast.24, s32[1,1]{1,0:T(1,128)S(6)} %copy.16.refs_3_, s32[1,256]{1,0:T(1,128)} %bitcast.25, s32[1,128]{1,0:T(1,128)} %refs_5_.1, f32[3,1,256]{2,1,0:T(1,128)} %bitcast.23, ...), custom_call_target="tpu_custom_call" | custom-call | tf_op jit(solution)/shard_map/step/pallas_call | solution.py:565
  47.2 0.0 copy-start
  47.2 1.7 %copy.17 = f32[19,1,32,128]{3,2,1,0:T(8,128)} copy(f32[19,1,32,128]{3,2,1,0:T(8,128)} %bitcast.17) | data formatting | bytes 622592
  48.9 0.0 copy-done
  48.9 0.7 %copy.18 = bf16[1,1,256,3,128]{4,2,3,1,0:T(8,128)(2,1)} copy(bf16[1,1,256,3,128]{4,2,3,1,0:T(8,128)(2,1)S(1)} %bitcast.19) | data formatting | bytes 393216
Async XLA Ops:
  47.2 1.8 %copy-start = (bf16[3,256,128]{2,1,0:T(8,128)(2,1)S(1)}, bf16[3,256,128]{2,1,0:T(8,128)(2,1)}, u32[]{:S(2)}) copy-start(bf16[3,256,128]{2,1,0:T(8,128)(2,1)} %get-tuple-element.5) | copy-start | bytes 589828

commit v4 on v3

--- a/solution.py
+++ b/solution.py
@@ -34,7 +34,7 @@
 SAMPLE_GROUP = 8
 SPREAD_GROUP = 16
 FIXED = float(1 << 21)
-VMEM_LIMIT = 60 * 1024 * 1024
+VMEM_LIMIT = 32 * 1024 * 1024
 X_UP = [i for i in range(19) if DIRS[i][0] == 1]
 X_DOWN = [i for i in range(19) if DIRS[i][0] == -1]
 Y_UP = [i for i in range(19) if DIRS[i][1] == 1]
@@ -199,13 +199,23 @@
     return 16 if lax.axis_size("slab") % 32 == 0 else 4
 
 
+def neighbours():
+    side = lax.axis_index("sub")
+    return side < lax.axis_size("sub") - 1, side > 0
+
+
 def greet():
     side = lax.axis_index("sub")
     barrier = pltpu.get_barrier_semaphore()
     for to in row_peers() + column_peers():
         pl.semaphore_signal(barrier, inc=1, **routed({"slab": to, "sub": side}))
-    for ids in near_ids()[:6]:
-        pl.semaphore_signal(barrier, inc=1, **routed(ids))
+    ids = near_ids()
+    for beside, chosen in zip(neighbours(), (ids[0:3], ids[3:6])):
+
+        @pl.when(beside)
+        def _():
+            for one in chosen:
+                pl.semaphore_signal(barrier, inc=1, **routed(one))
 
 
 def row_peers():
@@ -222,7 +232,9 @@
 def relay(row_sem):
     side = lax.axis_index("sub")
     rows, columns = row_peers(), column_peers()
-    pl.semaphore_wait(pltpu.get_barrier_semaphore(), len(rows) + len(columns) + 6)
+    last = lax.axis_size("sub") - 1
+    beside = (side + last - 1) // last + (2 * last - 1 - side) // last
+    pl.semaphore_wait(pltpu.get_barrier_semaphore(), len(rows) + len(columns) + 3 * beside)
     for to in columns:
         pl.semaphore_signal(row_sem, inc=1, **routed({"slab": to, "sub": side}))
 
@@ -357,22 +369,19 @@
     return jnp.broadcast_to(value[j : j + 1, :], (16, value.shape[1])).astype(BF16)
 
 
-def mark_depths(cell_ref, hot_ref, depth):
+def mark_depths(cell_ref, hot_ref, depth, half):
     slots, width = cell_ref.shape
-    lines = iota((16, width), 0).astype(F32).astype(BF16)
-    one, zero = jnp.ones((16, width), BF16), jnp.zeros((16, width), BF16)
+    lanes = iota((width, depth), 1).astype(F32)
 
     def block(g, carry):
-        z = split_cell(cell_ref[pl.ds(pl.multiple_of(g * 8, 8), 8), :], depth)[0].astype(F32)
+        z = split_cell(cell_ref[pl.ds(pl.multiple_of(g * 8, 8), 8), :], depth)[0].astype(F32).T
         for j in range(8):
-            zb = packed_row(z, j)
-            for i in range(depth // 16):
-                hot_ref[g, 16 * i : 16 * (i + 1), j * width : (j + 1) * width] = jnp.where(
-                    zb == lines + 16 * i, one, zero
-                )
+            hot_ref[g, j * width : (j + 1) * width, :] = ones_at(z[:, j : j + 1] == lanes)
         return carry
 
-    lax.fori_loop(0, slots // 8, block, 0)
+    steps = slots // 8
+    middle = steps // 2
+    lax.fori_loop(middle if half else 0, steps if half else middle, block, 0)
 
 
 def spread(cell_ref, force_ref, hot_ref, rows, depth):
@@ -396,7 +405,7 @@
                     vb = packed_row(vals[c], j)
                     stack += [jnp.where(mark, vb, zero) for mark in marks]
                 sides.append(jnp.concatenate(stack, axis=0))
-            total = total + dot(jnp.concatenate(sides, axis=1), hot_ref[g * group + n], NT)
+            total = total + dot(jnp.concatenate(sides, axis=1), hot_ref[g * group + n])
         return total
 
     return lax.fori_loop(0, slots // (8 * group), block, jnp.zeros((3 * rows, depth), F32))
@@ -481,7 +490,7 @@
         exchange_start(*there)
     with scope("p3_mark"):
         pair_columns(partner_ref, gap_ref, pairs_ref)
-        mark_depths(cell_ref, hot_ref, depth)
+        mark_depths(cell_ref, hot_ref, depth, 0)
     with scope("p4_wait"):
         exchange_wait(*there)
     with scope("p5_lub"):
@@ -489,6 +498,8 @@
     back = (reply_ref, returned_ref, bulk_sem.at[2], bulk_sem.at[3], own_sem.at[1], 6)
     with scope("p6_start"):
         exchange_start(*back)
+    with scope("p7_mark"):
+        mark_depths(cell_ref, hot_ref, depth, 1)
     with scope("p7_wait"):
         exchange_wait(*back)
     with scope("p8_unroute"):
@@ -508,14 +519,29 @@
             at = rows - 1 if DIRS[i][1] == 1 else 0
             edge_out_ref[n] = collided_ref[PLACE[i], at : at + 1, :]
     copies = halo_copies(collided_ref, x_low_ref, x_high_ref, edge_out_ref, edge_in_ref, halo_send, halo_recv)
-    for copy in copies:
+    for above, below in zip(copies[0:3], copies[3:6]):
+        pl.when(neighbours()[0])(above.start)
+        pl.when(neighbours()[1])(below.start)
+    for copy in copies[6:]:
         copy.start()
     streams = (collided_ref, x_low_ref, x_high_ref, edge_in_ref, read_ref)
     inner = [0, 5, 6]
     with scope("pc_inner"):
         stream(inner, *streams)
     with scope("pd_hwait"):
-        for copy in copies:
+        for above, below in zip(copies[0:3], copies[3:6]):
+
+            @pl.when(neighbours()[0])
+            def _():
+                above.wait_send()
+                below.wait_recv()
+
+            @pl.when(neighbours()[1])
+            def _():
+                below.wait_send()
+                above.wait_recv()
+
+        for copy in copies[6:]:
             copy.wait()
     with scope("pe_stream"):
         stream([i for i in range(19) if i not in inner], *streams)
@@ -558,7 +584,7 @@
         ((5, rows, depth), F32),
         ((10, 1, depth), F32),
         ((10, 1, depth), F32),
-        ((slots // 8, depth, 8 * width), BF16),
+        ((slots // 8, 8 * width, depth), BF16),
         ((slots, 8), F32),
     ]
     held = [(arg.shape, arg.dtype) for arg in args]
@@ -583,7 +609,7 @@
             collective_id=0, has_side_effects=True, vmem_limit_bytes=VMEM_LIMIT
         ),
         name="step",
-    )(*args)
+    )(*[pltpu.with_memory_space_constraint(arg, pltpu.HBM) if arg.size > 1 else arg for arg in args])
     return read[:, None], jnp.transpose(marker, (1, 0, 2))[None, None]
 
 

time: 49.8 us -> 46 us (0.924)
  the two profiles are of different devices: /device:TPU:1 before, /device:TPU:6 now
where the time goes in v4:
time: 46 us; the launch traced here: 45.4 us
  Pallas kernels  42.7 us (93%)
  local copies, waits for them, and re-layouts  1.4 us (3%)
  between operations  1.29 us (3%)
    pallas_call x1, Pallas kernels, per_device(): pl.pallas_call(step_kernel, out_shape=[jax.ShapeDtypeStruct((19, rows, de...  42.7 us
    unnamed x2, local copies, waits for them, and re-layouts  1.4 us

profile of v4, /device:TPU:6, one launch (start us, length us, event | category | flops | bytes accessed | tf_op | source)
XLA Modules:
  0.0 45.4 jit_solution(13554341745580061745)
XLA Ops:
  1.3 42.7 %step.1 = (f32[19,32,128]{2,1,0:T(8,128)S(1)}, bf16[3,256,128]{2,1,0:T(8,128)(2,1)S(1)}) custom-call(f32[19,32,128]{2,1,0:T(8,128)} %bitcast.19, s32[256,128]{1,0:T(8,128)} %bitcast.20, s32[1,256]{1,0:T(1,128)} %bitcast.24, s32[1,1]{1,0:T(1,128)S(6)} %copy.16.refs_3_, s32[1,256]{1,0:T(1,128)} %bitcast.25, s32[1,128]{1,0:T(1,128)} %refs_5_.1, ...), custom_call_target="tpu_custom_call" | custom-call | tf_op jit(solution)/shard_map/step/pallas_call | solution.py:591
  44.0 0.7 %copy.17 = f32[19,1,32,128]{3,2,1,0:T(8,128)} copy(f32[19,1,32,128]{3,2,1,0:T(8,128)S(1)} %bitcast.17) | data formatting | bytes 622592
  44.7 0.7 %copy.18 = bf16[1,1,256,3,128]{4,2,3,1,0:T(8,128)(2,1)} copy(bf16[1,1,256,3,128]{4,2,3,1,0:T(8,128)(2,1)S(1)} %bitcast.18) | data formatting | bytes 393216

commit v5 on v4

--- a/solution.py
+++ b/solution.py
@@ -97,10 +97,9 @@
 
 def slot_columns(velocity_ref, mcount_ref, pcount_ref, cols_ref):
     slots = mcount_ref.shape[1]
-    lim = jnp.where(iota((1, slots), 1) < pcount_ref[...], mcount_ref[...], 0).astype(F32)
-    stack = [velocity_ref[...].reshape(3, slots)] if velocity_ref is not None else [jnp.zeros((3, slots), F32)]
-    stack = jnp.concatenate(stack + [lim, jnp.zeros((4, slots), F32)], axis=0)
-    cols_ref[...] = stack.T
+    limit = jnp.where(iota((1, slots), 1) < pcount_ref[...], mcount_ref[...], 0).astype(F32)
+    stack = [velocity_ref[...].reshape(3, slots), limit, jnp.zeros((4, slots), F32)]
+    cols_ref[...] = jnp.concatenate(stack, axis=0).T
 
 
 def routes(pid_ref, table_ref, pcount_ref, width):
@@ -312,18 +311,22 @@
 
 def send_slip(refs):
     (cell_ref, mcount_ref, pcount_ref, pid_ref, table_ref, velocity_ref, pops_ref,
-     flow_ref, cols_ref, slip_ref, wide_ref, pick_ref, message_ref, row_sem) = refs
+     flow_ref, cols_ref, slip_ref, wide_ref, pick_ref, message_ref, row_sem, ready) = refs
     width = cell_ref.shape[1]
     slabs = message_ref.shape[0]
+    with scope("q0_load"):
+        ready(0, 5)
     with scope("q1_routes"):
         pick, spots = routes(pid_ref, table_ref, pcount_ref, width)
         pick_ref[...] = pick
         for p in range(2):
             wide_ref[pl.ds(6 + p, slabs, stride=8), :] = spots[p * slabs : (p + 1) * slabs]
+    with scope("q3_cols"):
+        slot_columns(velocity_ref, mcount_ref, pcount_ref, cols_ref)
+    with scope("q3_load"):
+        ready(5, 7)
     with scope("q2_flow"):
         flow_table(pops_ref, flow_ref)
-    with scope("q3_cols"):
-        slot_columns(velocity_ref, mcount_ref, pcount_ref, cols_ref)
     with scope("q4_sample"):
         sample(cell_ref, flow_ref, cols_ref, slip_ref, 0)
     with scope("q5_relay"):
@@ -465,7 +468,7 @@
 def step_kernel(*refs):
     given, (read_ref, marker_ref), rest = refs[:11], refs[11:13], refs[13:]
     held, rest = rest[:11], rest[11:]
-    (pops_ref, cell_ref, mcount_ref, pcount_ref, pid_ref, table_ref, velocity_ref,
+    (mcount_ref, pcount_ref, pid_ref, table_ref, velocity_ref, pops_ref, cell_ref,
      partner_ref, gap_ref, self_ref, pair_ref) = held
     (flow_ref, cols_ref, slip_ref, wide_ref, pick_ref, message_ref, got_ref, reply_ref, returned_ref,
      collided_ref, x_low_ref, x_high_ref, edge_out_ref, edge_in_ref, hot_ref, pairs_ref,
@@ -477,18 +480,21 @@
         load.start()
     with scope("p0_greet"):
         greet()
-    with scope("p0_load"):
-        for load in loads:
+
+    def ready(first, last):
+        for load in loads[first:last]:
             load.wait()
+
     with scope("p1_front"):
         send_slip((cell_ref, mcount_ref, pcount_ref, pid_ref, table_ref, velocity_ref, pops_ref,
-                   flow_ref, cols_ref, slip_ref, wide_ref, pick_ref, message_ref, row_sem))
+                   flow_ref, cols_ref, slip_ref, wide_ref, pick_ref, message_ref, row_sem, ready))
     with scope("p2_met"):
         met(row_sem)
     there = (message_ref, got_ref, bulk_sem.at[0], bulk_sem.at[1], own_sem.at[0], 8)
     with scope("p3_start"):
         exchange_start(*there)
     with scope("p3_mark"):
+        ready(7, 11)
         pair_columns(partner_ref, gap_ref, pairs_ref)
         mark_depths(cell_ref, hot_ref, depth, 0)
     with scope("p4_wait"):
@@ -547,6 +553,17 @@
         stream([i for i in range(19) if i not in inner], *streams)
 
 
+def emit_kernel(read_ref, marker_ref, read_out, marker_out, sem):
+    copies = [
+        pltpu.make_async_copy(read_ref, read_out, sem.at[0]),
+        pltpu.make_async_copy(marker_ref, marker_out, sem.at[1]),
+    ]
+    for copy in copies:
+        copy.start()
+    for copy in copies:
+        copy.wait()
+
+
 def per_device(
     populations, marker_cell, marker_count, particle_count, particle_id, owner_table,
     particle_velocity, pair_list, pair_gap, self_coupling, pair_coupling,
@@ -555,13 +572,13 @@
     slots, width = marker_cell.shape[2:]
     slabs = lax.axis_size("slab")
     args = (
-        populations[:, 0],
-        marker_cell[0, 0],
         marker_count[0],
         particle_count,
         particle_id[0],
         owner_table,
         jnp.transpose(particle_velocity[0], (1, 0, 2)),
+        populations[:, 0],
+        marker_cell[0, 0],
         jnp.transpose(pair_list[0, 0]),
         jnp.transpose(pair_gap[0, 0]),
         self_coupling,
@@ -610,6 +627,14 @@
         ),
         name="step",
     )(*[pltpu.with_memory_space_constraint(arg, pltpu.HBM) if arg.size > 1 else arg for arg in args])
+    read, marker = pl.pallas_call(
+        emit_kernel,
+        out_shape=[jax.ShapeDtypeStruct(part.shape, part.dtype) for part in (read, marker)],
+        in_specs=[pl.BlockSpec(memory_space=pl.ANY)] * 2,
+        out_specs=[pl.BlockSpec(memory_space=pl.ANY)] * 2,
+        scratch_shapes=[pltpu.SemaphoreType.DMA((2,))],
+        name="emit",
+    )(*[pltpu.with_memory_space_constraint(part, pltpu.VMEM) for part in (read, marker)])
     return read[:, None], jnp.transpose(marker, (1, 0, 2))[None, None]
 
 

time: 46 us -> 45.5 us (0.989)
  local copies, waits for them, and re-layouts: 1.4 us -> 0 us
  Pallas kernels: 42.7 us -> 43.5 us
    unnamed x2 -> x0, local copies, waits for them, and re-layouts: 1.4 us -> none
    pallas_call x0 -> x1, Pallas kernels: none -> 0.8 us  [per_device(): pl.pallas_call(emit_kernel, out_shape=[jax.ShapeDtypeStruct(part.shape, p...]
where the time goes in v5:
time: 45.5 us; the launch traced here: 44.8 us
  Pallas kernels  43.5 us (96%)
  between operations  1.29 us (3%)
    pallas_call x1, Pallas kernels, per_device(): pl.pallas_call(step_kernel, out_shape=[jax.ShapeDtypeStruct((19, rows, de...  42.7 us

profile of v5, /device:TPU:6, one launch (start us, length us, event | category | flops | bytes accessed | tf_op | source)
XLA Modules:
  0.0 44.8 jit_solution(1114653014776007167)
XLA Ops:
  1.3 42.7 %step.1 = (f32[19,32,128]{2,1,0:T(8,128)S(1)}, bf16[3,256,128]{2,1,0:T(8,128)(2,1)S(1)}) custom-call(s32[1,256]{1,0:T(1,128)} %bitcast.22, s32[1,1]{1,0:T(1,128)S(6)} %copy.14.refs_1_, s32[1,256]{1,0:T(1,128)} %bitcast.23, s32[1,128]{1,0:T(1,128)} %refs_3_.1, f32[3,1,256]{2,1,0:T(1,128)} %bitcast.21, f32[19,32,128]{2,1,0:T(8,128)} %bitcast.17, ...), custom_call_target="tpu_custom_call" | custom-call | tf_op jit(solution)/shard_map/step/pallas_call | solution.py:608
  44.0 0.8 %emit.1 = (f32[19,32,128]{2,1,0:T(8,128)}, bf16[3,256,128]{2,1,0:T(8,128)(2,1)}) custom-call(f32[19,32,128]{2,1,0:T(8,128)S(1)} %get-tuple-element.6.read_ref, bf16[3,256,128]{2,1,0:T(8,128)(2,1)S(1)} %get-tuple-element.7.marker_ref), custom_call_target="tpu_custom_call" | custom-call | tf_op jit(solution)/shard_map/emit/pallas_call | solution.py:630

commit v6 on v5

--- a/solution.py
+++ b/solution.py
@@ -32,7 +32,7 @@
 OPPOSITE = [0, 2, 1, 4, 3, 6, 5, 8, 7, 10, 9, 12, 11, 14, 13, 16, 15, 18, 17]
 OMEGA = 1.25
 SAMPLE_GROUP = 8
-SPREAD_GROUP = 16
+SPREAD_GROUP = 32
 FIXED = float(1 << 21)
 VMEM_LIMIT = 32 * 1024 * 1024
 X_UP = [i for i in range(19) if DIRS[i][0] == 1]

time: 45.5 us -> 45.3 us (level)
  no operation moved by 1% of the time
where the time goes in v6:
time: 45.3 us; the launch traced here: 44.5 us
  Pallas kernels  43.2 us (95%)
  between operations  1.29 us (3%)
    pallas_call x1, Pallas kernels, per_device(): pl.pallas_call(step_kernel, out_shape=[jax.ShapeDtypeStruct((19, rows, de...  42.4 us

profile of v6, /device:TPU:6, one launch (start us, length us, event | category | flops | bytes accessed | tf_op | source)
XLA Modules:
  0.0 44.5 jit_solution(3268959948344627206)
XLA Ops:
  1.3 42.4 %step.1 = (f32[19,32,128]{2,1,0:T(8,128)S(1)}, bf16[3,256,128]{2,1,0:T(8,128)(2,1)S(1)}) custom-call(s32[1,256]{1,0:T(1,128)} %bitcast.22, s32[1,1]{1,0:T(1,128)S(6)} %copy.14.refs_1_, s32[1,256]{1,0:T(1,128)} %bitcast.23, s32[1,128]{1,0:T(1,128)} %refs_3_.1, f32[3,1,256]{2,1,0:T(1,128)} %bitcast.21, f32[19,32,128]{2,1,0:T(8,128)} %bitcast.17, ...), custom_call_target="tpu_custom_call" | custom-call | tf_op jit(solution)/shard_map/step/pallas_call | solution.py:608
  43.7 0.8 %emit.1 = (f32[19,32,128]{2,1,0:T(8,128)}, bf16[3,256,128]{2,1,0:T(8,128)(2,1)}) custom-call(f32[19,32,128]{2,1,0:T(8,128)S(1)} %get-tuple-element.6.read_ref, bf16[3,256,128]{2,1,0:T(8,128)(2,1)S(1)} %get-tuple-element.7.marker_ref), custom_call_target="tpu_custom_call" | custom-call | tf_op jit(solution)/shard_map/emit/pallas_call | solution.py:630
